TPU v7x, 512 devices: a whole 4x8x8 slice. The times are simulated.
512 devices in a mesh: group: 4 (over z_hi), seq: 16 (over y, core), mp: 8 (over z_lo, x).
Axes of the slice: x: 4, y: 8, z: 8 (z_hi: 4, z_lo: 2; z = z_hi * 2 + z_lo), core: 2. Of those that a mesh axis runs over, the one named last changes fastest.
Arguments:
- patches: bfloat16 [32768, 640], P(('group', 'seq')), may hold values from -6 to 6
- w_merge1: bfloat16 [4, 640, 2560], P(None, 'seq', 'mp'), may hold values from -0.125 to 0.125
- w_merge2: bfloat16 [2560, 4096], P('mp', 'seq'), may hold values from -0.125 to 0.125
- w_query: bfloat16 [4096, 4096], P('seq', 'mp'), may hold values from -0.09375 to 0.09375
- w_keyval: bfloat16 [4096, 2, 1024], P('seq', None, 'mp'), may hold values from -0.09375 to 0.09375
- attn_grad: bfloat16 [8192, 4096], P(('group', 'seq'), 'mp'), may hold values from -6 to 6
- sample_ids: int32 [4, 2048], P('group'), may hold values from 0 to 7, never falling along the last dimension, each value on 1 to 1152 neighbouring positions
Outputs:
- patch_grad: bfloat16 [32768, 640], P(('group', 'seq', 'mp'))
Inputs may be any that keep to these rules, and one draw needn't show every extreme that they name: `sample_ids`: in each sequence never falls; every sample spans 1 to 1152 tokens.
All inputs are finite; a program needn't handle non-finite values.
Results may differ from a plain program's by a relative error of at most 0.035.
Values may be sent and summed in bfloat16 or wider, within the bound.
A program may use at most 64 MiB of HBM per device.

v0:
```python
import math

import jax
import jax.numpy as jnp
from jax import lax
from jax.sharding import PartitionSpec as P

HEAD = 128


EPSILON = 1e-06
NEGATIVE = 1e30


def shifted_2(value, axis, steps):
    count = lax.axis_size(axis)
    initial, last = (max(0, -steps), min(count, count - steps))
    return lax.ppermute(value, axis, [(source, source + steps) for source in range(initial, last)])


def copy_for_each(shard, axis):
    copies = jnp.broadcast_to(shard, (lax.axis_size(axis), *shard.shape))
    return lax.all_to_all(copies, axis, split_axis=0, concat_axis=0, tiled=True)


def laid_out(blocks, dim):
    blocks = jnp.moveaxis(blocks, 0, dim)
    lengths = blocks.shape
    return blocks.reshape(*lengths[:dim], lengths[dim] * lengths[dim + 1], *lengths[dim + 2 :])


def gather_directly(shard, axis, dim):
    blocks = copy_for_each(shard, axis)
    return laid_out(blocks, dim)


def split_up(shard, dim, peers):
    before, after = (shard.shape[:dim], shard.shape[dim + 1 :])
    return jnp.moveaxis(shard.reshape(*before, peers, -1, *after), dim, 0)


def sent_and_summed(shard, axis, dim):
    blocks = split_up(shard, dim, lax.axis_size(axis))
    arrived = lax.all_to_all(blocks, axis, split_axis=0, concat_axis=0, tiled=True)
    return arrived.astype(jnp.float32).sum(axis=0)


def side_by_side(arrays, axis, dim, along):
    widths = [math.prod(a.shape[along:]) for a in arrays]
    both = jnp.concatenate(
        [a.reshape(*a.shape[:along], w) for a, w in zip(arrays, widths)], axis=along
    )
    whole = lax.all_gather(both, axis, axis=dim, tiled=True)
    blocks = jnp.split(whole, [sum(widths[:k]) for k in range(1, len(widths))], axis=along)
    return tuple(
        (b.reshape(*whole.shape[:along], *a.shape[along:]) for a, b in zip(arrays, blocks))
    )


def gelu_grad(inputs):
    normal_cdf = 0.5 * (1.0 + lax.erf(inputs * 0.7071067811865476))
    normal_pdf = jnp.exp(-0.5 * inputs * inputs) * 0.3989422804014327
    return normal_cdf + inputs * normal_pdf


def fetch_earlier(own_keyval, offset):
    return shifted_2(own_keyval, "seq", offset)


def return_terms(terms, offset):
    return (
        shifted_2(terms[0].astype(jnp.bfloat16), "seq", -offset).astype(jnp.float32),
        shifted_2(terms[1].astype(jnp.bfloat16), "seq", -offset).astype(jnp.float32),
    )


def local(patches, w_merge1, w_merge2, w_query, w_keyval, attn_grad, sample_ids):
    patch_rows, feat_width = patches.shape
    tok_rows = patch_rows // 4
    score_scale = HEAD ** (-0.5)
    values = patches.astype(jnp.float32)
    row_mean = jnp.mean(values, -1, keepdims=True)
    ln_scale = lax.rsqrt(
        jnp.mean(values * values, -1, keepdims=True) - row_mean * row_mean + EPSILON
    )
    normed = (values - row_mean) * ln_scale
    merge_in = normed.astype(jnp.bfloat16).reshape(tok_rows, 4 * feat_width)
    first_tile = gather_directly(w_merge1, "seq", 1)
    first_flat = first_tile.reshape(4 * feat_width, first_tile.shape[2])
    hidden_pre = jnp.dot(merge_in, first_flat, preferred_element_type=jnp.float32)
    hidden = jax.nn.gelu(hidden_pre, approximate=False).astype(jnp.bfloat16)
    second_tile = lax.all_gather(w_merge2, "seq", axis=1, tiled=True)
    model_width = second_tile.shape[1]
    partial_value = jnp.dot(hidden, second_tile, preferred_element_type=jnp.float32)
    share = sent_and_summed(partial_value.astype(jnp.bfloat16), "mp", 0).astype(jnp.bfloat16)
    merged = gather_directly(share, "mp", 0)
    merged_f = merged.astype(jnp.float32)
    rms_scale = lax.rsqrt(jnp.mean(merged_f * merged_f, -1, keepdims=True) + EPSILON)
    normed_tok = merged_f * rms_scale
    query_tile, keyval_tile = side_by_side((w_query, w_keyval), "seq", 0, 1)
    kv_part = keyval_tile.shape[2]
    keyval_flat = keyval_tile.reshape(model_width, 2 * kv_part)
    normed_bf = normed_tok.astype(jnp.bfloat16)
    queries = jnp.dot(normed_bf, query_tile, preferred_element_type=jnp.float32).astype(
        jnp.bfloat16
    )
    own_keyval = jnp.dot(normed_bf, keyval_flat, preferred_element_type=jnp.float32).astype(
        jnp.bfloat16
    )
    query_part = queries.shape[1]
    kv_local = kv_part // HEAD
    per_kv = query_part // HEAD // kv_local
    run_ids = sample_ids[0]
    run_len = run_ids.shape[0]
    own_start = lax.axis_index("seq") * tok_rows
    reach = min(lax.axis_size("seq") - 1, (run_len // 2 + 2 * tok_rows - 2) // tok_rows)
    pieces = [own_keyval]
    for offset in range(1, reach + 1):
        pieces.insert(0, fetch_earlier(own_keyval, offset))
    window_kv = jnp.concatenate(pieces, 0)
    window_rows = window_kv.shape[0]
    key_pos = own_start - reach * tok_rows + jnp.arange(window_rows, dtype=jnp.int32)
    padded_ids = jnp.concatenate([jnp.full((reach * tok_rows,), -1, jnp.int32), run_ids], 0)
    key_ids = lax.dynamic_slice_in_dim(padded_ids, own_start, window_rows, 0)
    total_rows = window_kv.shape[0]
    key_heads = window_kv[:, :kv_part].reshape(total_rows, kv_local, HEAD)
    value_heads = window_kv[:, kv_part:].reshape(total_rows, kv_local, HEAD)
    query_pos = own_start + jnp.arange(tok_rows, dtype=jnp.int32)
    own_ids = lax.dynamic_slice_in_dim(run_ids, own_start, tok_rows, 0)
    allowed = (query_pos[:, None] >= key_pos[None, :]) & (own_ids[:, None] == key_ids[None, :])
    query_heads = queries.reshape(tok_rows, kv_local, per_kv, HEAD)
    scores = (
        jnp.einsum("tkgd,ukd->kgtu", query_heads, key_heads, preferred_element_type=jnp.float32)
        * score_scale
    )
    scores = jnp.where(allowed, scores, -NEGATIVE)
    row_max = jnp.max(scores, -1, keepdims=True)
    shifted = jnp.exp(scores - row_max)
    soft = shifted / jnp.sum(shifted, -1, keepdims=True)
    soft_bf = soft.astype(jnp.bfloat16)
    attended = jnp.einsum(
        "kgtu,ukd->tkgd", soft_bf, value_heads, preferred_element_type=jnp.float32
    )
    grad_heads = attn_grad.reshape(tok_rows, kv_local, per_kv, HEAD)
    row_delta = jnp.sum(grad_heads.astype(jnp.float32) * attended, -1)
    dprob = jnp.einsum(
        "tkgd,ukd->kgtu", grad_heads, value_heads, preferred_element_type=jnp.float32
    )
    dscore = (soft * (dprob - jnp.transpose(row_delta, (1, 2, 0))[..., None])).astype(jnp.bfloat16)
    dquery = (
        jnp.einsum("kgtu,ukd->tkgd", dscore, key_heads, preferred_element_type=jnp.float32)
        * score_scale
    )
    dquery = dquery.astype(jnp.bfloat16).reshape(tok_rows, query_part)
    dkey_terms = (
        jnp.einsum("kgtu,tkgd->ukd", dscore, query_heads, preferred_element_type=jnp.float32)
        * score_scale
    )
    dvalue_terms = jnp.einsum(
        "kgtu,tkgd->ukd", soft_bf, grad_heads, preferred_element_type=jnp.float32
    )
    dkey = dkey_terms[reach * tok_rows :]
    dvalue = dvalue_terms[reach * tok_rows :]
    for offset in range(1, reach + 1):
        begin_row = (reach - offset) * tok_rows
        key_back, value_back = return_terms(
            (
                dkey_terms[begin_row : begin_row + tok_rows],
                dvalue_terms[begin_row : begin_row + tok_rows],
            ),
            offset,
        )
        dkey = dkey + key_back
        dvalue = dvalue + value_back
    grads_kv = jnp.concatenate(
        [
            dkey.astype(jnp.bfloat16).reshape(tok_rows, kv_part),
            dvalue.astype(jnp.bfloat16).reshape(tok_rows, kv_part),
        ],
        1,
    )
    dnormed_part = jnp.einsum("tc,dc->td", dquery, query_tile, preferred_element_type=jnp.float32)
    dnormed_part = dnormed_part + jnp.einsum(
        "tc,dc->td", grads_kv, keyval_flat, preferred_element_type=jnp.float32
    )
    dnormed = lax.psum(dnormed_part.astype(jnp.bfloat16), "mp").astype(jnp.float32)
    inner_mean = jnp.mean(dnormed * normed_tok, -1, keepdims=True)
    dmerged = (rms_scale * (dnormed - normed_tok * inner_mean)).astype(jnp.bfloat16)
    dhidden = jnp.einsum("td,hd->th", dmerged, second_tile, preferred_element_type=jnp.float32)
    dhidden_pre = (dhidden * gelu_grad(hidden_pre)).astype(jnp.bfloat16)
    dmerge_part = jnp.einsum(
        "th,fh->tf", dhidden_pre, first_flat, preferred_element_type=jnp.float32
    )
    dmerge_in = sent_and_summed(
        dmerge_part.reshape(patch_rows, feat_width).astype(jnp.bfloat16), "mp", 0
    )
    share_rows = dmerge_in.shape[0]
    begin = lax.axis_index("mp") * share_rows
    own_normed = lax.dynamic_slice_in_dim(normed, begin, share_rows, 0)
    own_scale = lax.dynamic_slice_in_dim(ln_scale, begin, share_rows, 0)
    first_mean = jnp.mean(dmerge_in, -1, keepdims=True)
    second_mean = jnp.mean(dmerge_in * own_normed, -1, keepdims=True)
    patch_grad = own_scale * (dmerge_in - first_mean - own_normed * second_mean)
    return patch_grad.astype(jnp.bfloat16)


def solution(mesh):
    in_specs = (
        P(("group", "seq"), None),
        P(None, "seq", "mp"),
        P("mp", "seq"),
        P("seq", "mp"),
        P("seq", None, "mp"),
        P(("group", "seq"), "mp"),
        P("group", None),
    )
    out_specs = P(("group", "seq", "mp"), None)
    return jax.shard_map(local, mesh=mesh, in_specs=in_specs, out_specs=out_specs, check_vma=False)
```

profile of v0, /device:TPU:16, one launch (start us, length us, event | category | flops | bytes accessed | tf_op | source)
XLA Modules:
  0.0 370.7 jit_solution(3999455912178090720)
XLA Ops:
  10.0 2.3 broadcast_in_dim.10
  12.3 9.3 %all-to-all-start = ((bf16[16,4,40,320]{3,2,1,0:T(8,128)(2,1)}), bf16[16,4,40,320]{3,2,1,0:T(8,128)(2,1)S(1)}, u32[]{:S(2)}, u32[]{:S(2)}) async-start(bf16[16,4,40,320]{3,2,1,0:T(8,128)(2,1)} %broadcast_in_dim.10), calls=%async_computation | async-start | bytes 3932160 | tf_op jit(solution)/shard_map/all_to_all | solution.py:23
  25.1 49.2 %all-to-all-done = bf16[16,4,40,320]{3,2,1,0:T(8,128)(2,1)S(1)} async-done(((bf16[16,4,40,320]{3,2,1,0:T(8,128)(2,1)}), bf16[16,4,40,320]{3,2,1,0:T(8,128)(2,1)S(1)}, u32[]{:S(2)}, u32[]{:S(2)}) %all-to-all-start) | async-done | bytes 1638432 | tf_op jit(solution)/shard_map/all_to_all | solution.py:23
  78.2 6.8 %all-gather.3.cloned.1.call-done = bf16[320,4096]{1,0:T(8,128)(2,1)} async-done(((bf16[320,256]{1,0:T(8,128)(2,1)}), bf16[320,4096]{1,0:T(8,128)(2,1)}) %all-gather.3.cloned.1.call-update) | async-done | bytes 2621456 | tf_op jit(solution)/shard_map/all_gather | solution.py:92
  85.1 2.8 convolution_convert_fusion
  87.9 20.1 %all_to_all.20 = bf16[8,16,4096]{2,1,0:T(8,128)(2,1)S(1)} all-to-all(bf16[8,16,4096]{2,1,0:T(8,128)(2,1)S(1)} %bitcast.128), channel_id=1, replica_groups=mesh['group'=4,'seq'=16,'mp'=8] {'mp'}, dimensions={0} | all-to-all | bytes 2097152 | tf_op jit(solution)/shard_map/all_to_all | solution.py:44
  109.2 3.6 all-to-all-start.2
  115.3 11.5 %all-to-all-done.2 = bf16[8,16,4096]{2,1,0:T(8,128)(2,1)S(1)} async-done(((bf16[8,16,4096]{2,1,0:T(8,128)(2,1)}), bf16[8,16,4096]{2,1,0:T(8,128)(2,1)S(1)}, u32[]{:S(2)}, u32[]{:S(2)}) %all-to-all-start.2) | async-done | bytes 1048608 | tf_op jit(solution)/shard_map/all_to_all | solution.py:23
  128.4 9.3 %all-gather.5.cloned.1.call-done = bf16[4096,768]{1,0:T(8,128)(2,1)} async-done(((bf16[256,768]{1,0:T(8,128)(2,1)}), bf16[4096,768]{1,0:T(8,128)(2,1)}) %all-gather.5.cloned.1.call-update) | async-done | bytes 6291472 | tf_op jit(solution)/shard_map/all_gather | solution.py:53
  137.6 3.1 fusion.41
  142.8 3.4 collective-permute-start.7
  146.3 3.2 collective-permute-start.6
  149.5 3.3 collective-permute-start.5
  154.7 2.9 fusion.33
  157.8 7.7 %collective-permute-start.1 = (bf16[128,256]{1,0:T(8,128)(2,1)}, bf16[128,256]{1,0:T(8,128)(2,1)S(1)}, u32[]{:S(2)}, u32[]{:S(2)}) collective-permute-start(bf16[128,256]{1,0:T(8,128)(2,1)} %fusion.41), channel_id=1, source_target_pairs={{0,64},{8,72},{16,80},{24,88},{32,96},{40,104},{48,112},{56,120},{... | collective-permute-start | bytes 196616 | tf_op jit(solution)/shard_map/ppermute | solution.py:18
  168.3 6.7 %collective-permute-start.2 = (bf16[128,256]{1,0:T(8,128)(2,1)}, bf16[128,256]{1,0:T(8,128)(2,1)S(1)}, u32[]{:S(2)}, u32[]{:S(2)}) collective-permute-start(bf16[128,256]{1,0:T(8,128)(2,1)} %fusion.41), channel_id=1, source_target_pairs={{0,56},{8,64},{16,72},{24,80},{32,88},{40,96},{48,104},{56,112},{6... | collective-permute-start | bytes 196616 | tf_op jit(solution)/shard_map/ppermute | solution.py:18
  175.1 2.4 collective-permute-done.2
  177.5 8.9 %collective-permute-start.3 = (bf16[128,256]{1,0:T(8,128)(2,1)}, bf16[128,256]{1,0:T(8,128)(2,1)S(1)}, u32[]{:S(2)}, u32[]{:S(2)}) collective-permute-start(bf16[128,256]{1,0:T(8,128)(2,1)} %fusion.41), channel_id=1, source_target_pairs={{0,48},{8,56},{16,64},{24,72},{32,80},{40,88},{48,96},{56,104},{64... | collective-permute-start | bytes 196616 | tf_op jit(solution)/shard_map/ppermute | solution.py:18
  190.7 2.5 collective-permute-done.4
  211.1 5.9 %collective-permute-done.17 = bf16[128,1,128]{0,2,1:T(8,128)(2,1)S(1)} collective-permute-done((bf16[128,1,128]{0,2,1:T(8,128)(2,1)S(1)}, bf16[128,1,128]{0,2,1:T(8,128)(2,1)S(1)}, u32[]{:S(2)}, u32[]{:S(2)}) %collective-permute-start.17) | collective-permute-done | bytes 32800 | tf_op jit(solution)/shard_map/ppermute | solution.py:18
  248.5 91.3 %all-reduce.3.cloned.1.call-done = bf16[128,4096]{1,0:T(8,128)(2,1)} async-done(((bf16[128,4096]{1,0:T(8,128)(2,1)}), bf16[128,4096]{1,0:T(8,128)(2,1)}) %all-reduce.3.cloned.1.call-update) | async-done | bytes 1048592 | tf_op jit(solution)/shard_map/psum | solution.py:186
  343.1 4.5 %convolution_convert_fusion.1 = bf16[128,2560]{1,0:T(8,128)(2,1)S(1)} fusion(bf16[2560,320]{1,0:T(8,128)(2,1)S(1)} %bitcast.122, bf16[128,4096]{1,0:T(8,128)(2,1)} %fusion.17, bf16[320,4096]{1,0:T(8,128)(2,1)} %all-gather.3.cloned.1.call-done, f32[128,320]{0,1:T(8,128)S(1)} %copy-done.5), kind=kOutput, calls=%fused_computation.7 | convolution fusion | flops 545996800 | bytes 6127616 | tf_op jit(solution)/shard_map/th,fh->tf/dot_general | solution.py:191
  348.9 3.5 all-to-all-start.3
  352.5 8.7 %all-to-all-done.3 = bf16[8,64,640]{2,1,0:T(8,128)(2,1)S(1)} async-done(((bf16[8,64,640]{2,1,0:T(8,128)(2,1)}), bf16[8,64,640]{2,1,0:T(8,128)(2,1)S(1)}, u32[]{:S(2)}, u32[]{:S(2)}) %all-to-all-start.3) | async-done | bytes 655392 | tf_op jit(solution)/shard_map/all_to_all | solution.py:44
  (129 shorter events, 83.9 us)
Async XLA Ops:
  6.5 78.5 %all-gather.3.cloned.1.call-start = ((), (), s32[]{:S(2)}) async-start(), calls=%async_computation.4 | async-start | bytes 2785280 | tf_op jit(solution)/shard_map/all_gather | solution.py:92
  7.3 130.4 %all-gather.5.cloned.1.call-start = ((), (), s32[]{:S(2)}) async-start(), calls=%async_computation.5 | async-start | bytes 6684672 | tf_op jit(solution)/shard_map/all_gather | solution.py:53
  12.3 62.0 %all-to-all-start = ((bf16[16,4,40,320]{3,2,1,0:T(8,128)(2,1)}), bf16[16,4,40,320]{3,2,1,0:T(8,128)(2,1)S(1)}, u32[]{:S(2)}, u32[]{:S(2)}) async-start(bf16[16,4,40,320]{3,2,1,0:T(8,128)(2,1)} %broadcast_in_dim.10), calls=%async_computation | async-start | bytes 3932160 | tf_op jit(solution)/shard_map/all_to_all | solution.py:23
  109.2 17.6 %all-to-all-start.2 = ((bf16[8,16,4096]{2,1,0:T(8,128)(2,1)}), bf16[8,16,4096]{2,1,0:T(8,128)(2,1)S(1)}, u32[]{:S(2)}, u32[]{:S(2)}) async-start(bf16[8,16,4096]{2,1,0:T(8,128)(2,1)} %broadcast_in_dim.11), calls=%async_computation.2 | async-start | bytes 2097152 | tf_op jit(solution)/shard_map/all_to_all | solution.py:23
  112.8 227.0 %all-reduce.3.cloned.1.call-start = ((), (), s32[]{:S(2)}) async-start(), calls=%async_computation.6 | async-start | bytes 2097152 | tf_op jit(solution)/shard_map/psum | solution.py:186
  140.7 55.1 %collective-permute-start.8 = (bf16[128,256]{1,0:T(8,128)(2,1)}, bf16[128,256]{1,0:T(8,128)(2,1)}, u32[]{:S(2)}, u32[]{:S(2)}) collective-permute-start(bf16[128,256]{1,0:T(8,128)(2,1)} %fusion.41), channel_id=1, source_target_pairs={{0,8},{8,16},{16,24},{24,32},{32,40},{40,48},{48,56},{56,64},{64,7... | collective-permute-start | bytes 196616 | tf_op jit(solution)/shard_map/ppermute | solution.py:18
  142.8 52.1 %collective-permute-start.7 = (bf16[128,256]{1,0:T(8,128)(2,1)}, bf16[128,256]{1,0:T(8,128)(2,1)}, u32[]{:S(2)}, u32[]{:S(2)}) collective-permute-start(bf16[128,256]{1,0:T(8,128)(2,1)} %fusion.41), channel_id=1, source_target_pairs={{0,16},{8,24},{16,32},{24,40},{32,48},{40,56},{48,64},{56,72},{64,... | collective-permute-start | bytes 196616 | tf_op jit(solution)/shard_map/ppermute | solution.py:18
  146.3 47.9 %collective-permute-start.6 = (bf16[128,256]{1,0:T(8,128)(2,1)}, bf16[128,256]{1,0:T(8,128)(2,1)}, u32[]{:S(2)}, u32[]{:S(2)}) collective-permute-start(bf16[128,256]{1,0:T(8,128)(2,1)} %fusion.41), channel_id=1, source_target_pairs={{0,24},{8,32},{16,40},{24,48},{32,56},{40,64},{48,72},{56,80},{64,... | collective-permute-start | bytes 196616 | tf_op jit(solution)/shard_map/ppermute | solution.py:18
  149.5 43.8 %collective-permute-start.5 = (bf16[128,256]{1,0:T(8,128)(2,1)}, bf16[128,256]{1,0:T(8,128)(2,1)}, u32[]{:S(2)}, u32[]{:S(2)}) collective-permute-start(bf16[128,256]{1,0:T(8,128)(2,1)} %fusion.41), channel_id=1, source_target_pairs={{0,32},{8,40},{16,48},{24,56},{32,64},{40,72},{48,80},{56,88},{64,... | collective-permute-start | bytes 196616 | tf_op jit(solution)/shard_map/ppermute | solution.py:18
  157.8 10.6 %collective-permute-start.1 = (bf16[128,256]{1,0:T(8,128)(2,1)}, bf16[128,256]{1,0:T(8,128)(2,1)S(1)}, u32[]{:S(2)}, u32[]{:S(2)}) collective-permute-start(bf16[128,256]{1,0:T(8,128)(2,1)} %fusion.41), channel_id=1, source_target_pairs={{0,64},{8,72},{16,80},{24,88},{32,96},{40,104},{48,112},{56,120},{... | collective-permute-start | bytes 196616 | tf_op jit(solution)/shard_map/ppermute | solution.py:18
  177.5 11.1 %collective-permute-start.3 = (bf16[128,256]{1,0:T(8,128)(2,1)}, bf16[128,256]{1,0:T(8,128)(2,1)S(1)}, u32[]{:S(2)}, u32[]{:S(2)}) collective-permute-start(bf16[128,256]{1,0:T(8,128)(2,1)} %fusion.41), channel_id=1, source_target_pairs={{0,48},{8,56},{16,64},{24,72},{32,80},{40,88},{48,96},{56,104},{64... | collective-permute-start | bytes 196616 | tf_op jit(solution)/shard_map/ppermute | solution.py:18
  204.2 12.8 %collective-permute-start.17 = (bf16[128,1,128]{0,2,1:T(8,128)(2,1)S(1)}, bf16[128,1,128]{0,2,1:T(8,128)(2,1)S(1)}, u32[]{:S(2)}, u32[]{:S(2)}) collective-permute-start(bf16[128,1,128]{0,2,1:T(8,128)(2,1)S(1)} %get-tuple-element.12), channel_id=1, source_target_pairs={{72,0},{80,8},{88,16},{96,24},{104,32},{112,40},{120,48},{73,1},{8... | collective-permute-start | bytes 98312 | tf_op jit(solution)/shard_map/ppermute | solution.py:18
  205.5 13.4 %collective-permute-start.16 = (bf16[128,1,128]{0,2,1:T(8,128)(2,1)S(1)}, bf16[128,1,128]{0,2,1:T(8,128)(2,1)S(1)}, u32[]{:S(2)}, u32[]{:S(2)}) collective-permute-start(bf16[128,1,128]{0,2,1:T(8,128)(2,1)S(1)} %get-tuple-element.13), channel_id=1, source_target_pairs={{64,0},{72,8},{80,16},{88,24},{96,32},{104,40},{112,48},{120,56},{... | collective-permute-start | bytes 98312 | tf_op jit(solution)/shard_map/ppermute | solution.py:18
  207.2 13.7 %collective-permute-start.15 = (bf16[128,1,128]{0,2,1:T(8,128)(2,1)S(1)}, bf16[128,1,128]{0,2,1:T(8,128)(2,1)S(1)}, u32[]{:S(2)}, u32[]{:S(2)}) collective-permute-start(bf16[128,1,128]{0,2,1:T(8,128)(2,1)S(1)} %get-tuple-element.14), channel_id=1, source_target_pairs={{56,0},{64,8},{72,16},{80,24},{88,32},{96,40},{104,48},{112,56},{1... | collective-permute-start | bytes 98312 | tf_op jit(solution)/shard_map/ppermute | solution.py:18
  208.5 16.5 %collective-permute-start.14 = (bf16[128,1,128]{0,2,1:T(8,128)(2,1)S(1)}, bf16[128,1,128]{0,2,1:T(8,128)(2,1)S(1)}, u32[]{:S(2)}, u32[]{:S(2)}) collective-permute-start(bf16[128,1,128]{0,2,1:T(8,128)(2,1)S(1)} %get-tuple-element.15), channel_id=1, source_target_pairs={{48,0},{56,8},{64,16},{72,24},{80,32},{88,40},{96,48},{104,56},{11... | collective-permute-start | bytes 98312 | tf_op jit(solution)/shard_map/ppermute | solution.py:18
  209.8 17.1 %collective-permute-start.13 = (bf16[128,1,128]{0,2,1:T(8,128)(2,1)S(1)}, bf16[128,1,128]{0,2,1:T(8,128)(2,1)S(1)}, u32[]{:S(2)}, u32[]{:S(2)}) collective-permute-start(bf16[128,1,128]{0,2,1:T(8,128)(2,1)S(1)} %get-tuple-element.16), channel_id=1, source_target_pairs={{40,0},{48,8},{56,16},{64,24},{72,32},{80,40},{88,48},{96,56},{104... | collective-permute-start | bytes 98312 | tf_op jit(solution)/shard_map/ppermute | solution.py:18
  217.0 11.2 %collective-permute-start.12 = (bf16[128,1,128]{0,2,1:T(8,128)(2,1)S(1)}, bf16[128,1,128]{0,2,1:T(8,128)(2,1)S(1)}, u32[]{:S(2)}, u32[]{:S(2)}) collective-permute-start(bf16[128,1,128]{0,2,1:T(8,128)(2,1)S(1)} %get-tuple-element.17), channel_id=1, source_target_pairs={{32,0},{40,8},{48,16},{56,24},{64,32},{72,40},{80,48},{88,56},{96,... | collective-permute-start | bytes 98312 | tf_op jit(solution)/shard_map/ppermute | solution.py:18
  218.9 10.6 %collective-permute-start.11 = (bf16[128,1,128]{0,2,1:T(8,128)(2,1)S(1)}, bf16[128,1,128]{0,2,1:T(8,128)(2,1)S(1)}, u32[]{:S(2)}, u32[]{:S(2)}) collective-permute-start(bf16[128,1,128]{0,2,1:T(8,128)(2,1)S(1)} %get-tuple-element.18), channel_id=1, source_target_pairs={{24,0},{32,8},{40,16},{48,24},{56,32},{64,40},{72,48},{80,56},{88,... | collective-permute-start | bytes 98312 | tf_op jit(solution)/shard_map/ppermute | solution.py:18
  220.9 11.6 %collective-permute-start.10 = (bf16[128,1,128]{0,2,1:T(8,128)(2,1)S(1)}, bf16[128,1,128]{0,2,1:T(8,128)(2,1)S(1)}, u32[]{:S(2)}, u32[]{:S(2)}) collective-permute-start(bf16[128,1,128]{0,2,1:T(8,128)(2,1)S(1)} %get-tuple-element.19), channel_id=1, source_target_pairs={{16,0},{24,8},{32,16},{40,24},{48,32},{56,40},{64,48},{72,56},{80,... | collective-permute-start | bytes 98312 | tf_op jit(solution)/shard_map/ppermute | solution.py:18
  226.9 10.1 %collective-permute-start.26 = (bf16[128,1,128]{0,2,1:T(8,128)(2,1)S(1)}, bf16[128,1,128]{0,2,1:T(8,128)(2,1)S(1)}, u32[]{:S(2)}, u32[]{:S(2)}) collective-permute-start(bf16[128,1,128]{0,2,1:T(8,128)(2,1)S(1)} %get-tuple-element.21), channel_id=1, source_target_pairs={{72,0},{80,8},{88,16},{96,24},{104,32},{112,40},{120,48},{73,1},{8... | collective-permute-start | bytes 98312 | tf_op jit(solution)/shard_map/ppermute | solution.py:18
  228.2 10.7 %collective-permute-start.25 = (bf16[128,1,128]{0,2,1:T(8,128)(2,1)S(1)}, bf16[128,1,128]{0,2,1:T(8,128)(2,1)S(1)}, u32[]{:S(2)}, u32[]{:S(2)}) collective-permute-start(bf16[128,1,128]{0,2,1:T(8,128)(2,1)S(1)} %get-tuple-element.22), channel_id=1, source_target_pairs={{64,0},{72,8},{80,16},{88,24},{96,32},{104,40},{112,48},{120,56},{... | collective-permute-start | bytes 98312 | tf_op jit(solution)/shard_map/ppermute | solution.py:18
  229.5 11.3 %collective-permute-start.24 = (bf16[128,1,128]{0,2,1:T(8,128)(2,1)S(1)}, bf16[128,1,128]{0,2,1:T(8,128)(2,1)S(1)}, u32[]{:S(2)}, u32[]{:S(2)}) collective-permute-start(bf16[128,1,128]{0,2,1:T(8,128)(2,1)S(1)} %get-tuple-element.23), channel_id=1, source_target_pairs={{56,0},{64,8},{72,16},{80,24},{88,32},{96,40},{104,48},{112,56},{1... | collective-permute-start | bytes 98312 | tf_op jit(solution)/shard_map/ppermute | solution.py:18
  232.5 10.3 %collective-permute-start.23 = (bf16[128,1,128]{0,2,1:T(8,128)(2,1)S(1)}, bf16[128,1,128]{0,2,1:T(8,128)(2,1)S(1)}, u32[]{:S(2)}, u32[]{:S(2)}) collective-permute-start(bf16[128,1,128]{0,2,1:T(8,128)(2,1)S(1)} %get-tuple-element.24), channel_id=1, source_target_pairs={{48,0},{56,8},{64,16},{72,24},{80,32},{88,40},{96,48},{104,56},{11... | collective-permute-start | bytes 98312 | tf_op jit(solution)/shard_map/ppermute | solution.py:18
  348.9 12.3 %all-to-all-start.3 = ((bf16[8,64,640]{2,1,0:T(8,128)(2,1)}), bf16[8,64,640]{2,1,0:T(8,128)(2,1)S(1)}, u32[]{:S(2)}, u32[]{:S(2)}) async-start(bf16[8,64,640]{2,1,0:T(8,128)(2,1)} %convert_element_type.206), calls=%async_computation.3 | async-start | bytes 1310720 | tf_op jit(solution)/shard_map/all_to_all | solution.py:44
  (20 other events, 176.9 us)
Sparse Core Ops, SparseCore 0:
  9.4 75.6 all-gather.2
  87.2 50.4 all-gather.4
  248.6 91.0 all-reduce.2
where the time goes:
time: 372 us; the launch traced here: 371 us
  waiting for transfers between devices  200 us (54%)
  starting transfers between devices  84.9 us (23%)
  matrix products  21.5 us (6%)
  blocking collectives  20.1 us (5%)
  local copies, waits for them, and re-layouts  16.6 us (4%)
  other arithmetic  14 us (4%)
  between operations  13.8 us (4%)
    psum x1, waiting for transfers between devices, local(): lax.psum(dnormed_part.astype(jnp.bfloat16), 'mp').astype(jnp.float32)  91.3 us
    ppermute x27, starting transfers between devices, shifted_2(): lax.ppermute(value, axis, [(source, source + steps) for source in range(i...  68.4 us
    all_to_all x2, waiting for transfers between devices, copy_for_each(): return lax.all_to_all(copies, axis, split_axis=0, concat_axis=0, tiled=True)  60.7 us
    ppermute x27, waiting for transfers between devices, shifted_2(): lax.ppermute(value, axis, [(source, source + steps) for source in range(i...  22.3 us
    all_to_all x1, blocking collectives, sent_and_summed(): lax.all_to_all(blocks, axis, split_axis=0, concat_axis=0, tiled=True)  20.1 us
    all_to_all x2, starting transfers between devices, copy_for_each(): return lax.all_to_all(copies, axis, split_axis=0, concat_axis=0, tiled=True)  12.9 us
    all_gather x1, waiting for transfers between devices, side_by_side(): whole = lax.all_gather(both, axis, axis=dim, tiled=True)  9.25 us
    all_to_all x1, waiting for transfers between devices, sent_and_summed(): lax.all_to_all(blocks, axis, split_axis=0, concat_axis=0, tiled=True)  8.68 us
  transfers between devices with their start and end apart: 33, of which 15 were waited for; matrix products, arithmetic and copies ran while one was open for 7% of the time, Pallas kernels for 0%

commit v1 on v0

--- a/solution.py
+++ b/solution.py
@@ -183,9 +183,14 @@
     dnormed_part = dnormed_part + jnp.einsum(
         "tc,dc->td", grads_kv, keyval_flat, preferred_element_type=jnp.float32
     )
-    dnormed = lax.psum(dnormed_part.astype(jnp.bfloat16), "mp").astype(jnp.float32)
-    inner_mean = jnp.mean(dnormed * normed_tok, -1, keepdims=True)
-    dmerged = (rms_scale * (dnormed - normed_tok * inner_mean)).astype(jnp.bfloat16)
+    dnormed = sent_and_summed(dnormed_part.astype(jnp.bfloat16), "mp", 0)
+    own_rows = dnormed.shape[0]
+    row_start = lax.axis_index("mp") * own_rows
+    own_tok = lax.dynamic_slice_in_dim(normed_tok, row_start, own_rows, 0)
+    own_rms = lax.dynamic_slice_in_dim(rms_scale, row_start, own_rows, 0)
+    inner_mean = jnp.mean(dnormed * own_tok, -1, keepdims=True)
+    dmerged_share = (own_rms * (dnormed - own_tok * inner_mean)).astype(jnp.bfloat16)
+    dmerged = gather_directly(dmerged_share, "mp", 0)
     dhidden = jnp.einsum("td,hd->th", dmerged, second_tile, preferred_element_type=jnp.float32)
     dhidden_pre = (dhidden * gelu_grad(hidden_pre)).astype(jnp.bfloat16)
     dmerge_part = jnp.einsum(

time: 372 us -> 313 us (0.84)
  the two profiles are of different devices: /device:TPU:16 before, /device:TPU:48 now
where the time goes in v1:
time: 313 us; the launch traced here: 312 us
  waiting for transfers between devices  144 us (46%)
  starting transfers between devices  72.6 us (23%)
  blocking collectives  40.4 us (13%)
  matrix products  19.8 us (6%)
  between operations  14.2 us (5%)
  local copies, waits for them, and re-layouts  10.8 us (3%)
  other arithmetic  9.84 us (3%)
    all_to_all x2, waiting for transfers between devices, copy_for_each(): return lax.all_to_all(copies, axis, split_axis=0, concat_axis=0, tiled=True)  63.7 us
    ppermute x27, starting transfers between devices, shifted_2(): lax.ppermute(value, axis, [(source, source + steps) for source in range(i...  51.2 us
    ppermute x27, waiting for transfers between devices, shifted_2(): lax.ppermute(value, axis, [(source, source + steps) for source in range(i...  42.2 us
    all_to_all x2, waiting for transfers between devices, sent_and_summed(): lax.all_to_all(blocks, axis, split_axis=0, concat_axis=0, tiled=True)  24 us
    all_to_all x1, blocking collectives, sent_and_summed(): lax.all_to_all(blocks, axis, split_axis=0, concat_axis=0, tiled=True)  21 us
    all_to_all x1, blocking collectives, copy_for_each(): return lax.all_to_all(copies, axis, split_axis=0, concat_axis=0, tiled=True)  19.4 us
    all_to_all x2, starting transfers between devices, copy_for_each(): return lax.all_to_all(copies, axis, split_axis=0, concat_axis=0, tiled=True)  12.5 us
    all_to_all x2, starting transfers between devices, sent_and_summed(): lax.all_to_all(blocks, axis, split_axis=0, concat_axis=0, tiled=True)  8.87 us
  transfers between devices with their start and end apart: 33, of which 12 were waited for; matrix products, arithmetic and copies ran while one was open for 7% of the time, Pallas kernels for 0%

profile of v1, /device:TPU:48, one launch (start us, length us, event | category | flops | bytes accessed | tf_op | source)
XLA Modules:
  0.0 311.7 jit_solution(8116721710496433510)
XLA Ops:
  12.3 8.9 %all-to-all-start = ((bf16[16,4,40,320]{3,2,1,0:T(8,128)(2,1)}), bf16[16,4,40,320]{3,2,1,0:T(8,128)(2,1)S(1)}, u32[]{:S(2)}, u32[]{:S(2)}) async-start(bf16[16,4,40,320]{3,2,1,0:T(8,128)(2,1)} %broadcast_in_dim.14), calls=%async_computation | async-start | bytes 3932160 | tf_op jit(solution)/shard_map/all_to_all | solution.py:23
  23.3 52.2 %all-to-all-done = bf16[16,4,40,320]{3,2,1,0:T(8,128)(2,1)S(1)} async-done(((bf16[16,4,40,320]{3,2,1,0:T(8,128)(2,1)}), bf16[16,4,40,320]{3,2,1,0:T(8,128)(2,1)S(1)}, u32[]{:S(2)}, u32[]{:S(2)}) %all-to-all-start) | async-done | bytes 1638432 | tf_op jit(solution)/shard_map/all_to_all | solution.py:23
  79.4 4.5 %all-gather.3.cloned.1.call-done = bf16[320,4096]{1,0:T(8,128)(2,1)} async-done(((bf16[320,256]{1,0:T(8,128)(2,1)}), bf16[320,4096]{1,0:T(8,128)(2,1)}) %all-gather.3.cloned.1.call-update) | async-done | bytes 2621456 | tf_op jit(solution)/shard_map/all_gather | solution.py:92
  83.9 2.8 convolution_convert_fusion
  86.8 21.0 %all_to_all.30 = bf16[8,16,4096]{2,1,0:T(8,128)(2,1)S(1)} all-to-all(bf16[8,16,4096]{2,1,0:T(8,128)(2,1)S(1)} %bitcast.126), channel_id=1, replica_groups=mesh['group'=4,'seq'=16,'mp'=8] {'mp'}, dimensions={0} | all-to-all | bytes 2097152 | tf_op jit(solution)/shard_map/all_to_all | solution.py:44
  109.1 3.6 %all-to-all-start.2 = ((bf16[8,16,4096]{2,1,0:T(8,128)(2,1)}), bf16[8,16,4096]{2,1,0:T(8,128)(2,1)S(1)}, u32[]{:S(2)}, u32[]{:S(2)}) async-start(bf16[8,16,4096]{2,1,0:T(8,128)(2,1)} %broadcast_in_dim.15), calls=%async_computation.2 | async-start | bytes 2097152 | tf_op jit(solution)/shard_map/all_to_all | solution.py:23
  115.1 11.5 %all-to-all-done.2 = bf16[8,16,4096]{2,1,0:T(8,128)(2,1)S(1)} async-done(((bf16[8,16,4096]{2,1,0:T(8,128)(2,1)}), bf16[8,16,4096]{2,1,0:T(8,128)(2,1)S(1)}, u32[]{:S(2)}, u32[]{:S(2)}) %all-to-all-start.2) | async-done | bytes 1048608 | tf_op jit(solution)/shard_map/all_to_all | solution.py:23
  127.3 8.8 %all-gather.5.cloned.1.call-done = bf16[4096,768]{1,0:T(8,128)(2,1)} async-done(((bf16[256,768]{1,0:T(8,128)(2,1)}), bf16[4096,768]{1,0:T(8,128)(2,1)}) %all-gather.5.cloned.1.call-update) | async-done | bytes 6291472 | tf_op jit(solution)/shard_map/all_gather | solution.py:53
  140.4 3.3 %collective-permute-start.7 = (bf16[128,256]{1,0:T(8,128)(2,1)S(1)}, bf16[128,256]{1,0:T(8,128)(2,1)S(1)}, u32[]{:S(2)}, u32[]{:S(2)}) collective-permute-start(bf16[128,256]{1,0:T(8,128)(2,1)S(1)} %fusion.37), channel_id=1, source_target_pairs={{0,16},{8,24},{16,32},{24,40},{32,48},{40,56},{48,64},{56,72},{64,... | collective-permute-start | bytes 196616 | tf_op jit(solution)/shard_map/ppermute | solution.py:18
  148.2 2.9 fusion.29
  151.3 4.7 %collective-permute-done = bf16[128,256]{1,0:T(8,128)(2,1)S(1)} collective-permute-done((bf16[128,256]{1,0:T(8,128)(2,1)S(1)}, bf16[128,256]{1,0:T(8,128)(2,1)S(1)}, u32[]{:S(2)}, u32[]{:S(2)}) %collective-permute-start) | collective-permute-done | bytes 65568 | tf_op jit(solution)/shard_map/ppermute | solution.py:18
  157.2 8.8 %collective-permute-done.1 = bf16[128,256]{1,0:T(8,128)(2,1)S(1)} collective-permute-done((bf16[128,256]{1,0:T(8,128)(2,1)S(1)}, bf16[128,256]{1,0:T(8,128)(2,1)S(1)}, u32[]{:S(2)}, u32[]{:S(2)}) %collective-permute-start.1) | collective-permute-done | bytes 65568 | tf_op jit(solution)/shard_map/ppermute | solution.py:18
  167.3 8.2 %collective-permute-done.2 = bf16[128,256]{1,0:T(8,128)(2,1)S(1)} collective-permute-done((bf16[128,256]{1,0:T(8,128)(2,1)S(1)}, bf16[128,256]{1,0:T(8,128)(2,1)S(1)}, u32[]{:S(2)}, u32[]{:S(2)}) %collective-permute-start.2) | collective-permute-done | bytes 65568 | tf_op jit(solution)/shard_map/ppermute | solution.py:18
  176.8 9.8 %collective-permute-done.3 = bf16[128,256]{1,0:T(8,128)(2,1)S(1)} collective-permute-done((bf16[128,256]{1,0:T(8,128)(2,1)S(1)}, bf16[128,256]{1,0:T(8,128)(2,1)S(1)}, u32[]{:S(2)}, u32[]{:S(2)}) %collective-permute-start.3) | collective-permute-done | bytes 65568 | tf_op jit(solution)/shard_map/ppermute | solution.py:18
  187.9 7.5 %collective-permute-done.4 = bf16[128,256]{1,0:T(8,128)(2,1)S(1)} collective-permute-done((bf16[128,256]{1,0:T(8,128)(2,1)S(1)}, bf16[128,256]{1,0:T(8,128)(2,1)S(1)}, u32[]{:S(2)}, u32[]{:S(2)}) %collective-permute-start.4) | collective-permute-done | bytes 65568 | tf_op jit(solution)/shard_map/ppermute | solution.py:18
  211.5 4.3 %collective-permute-start.11 = (bf16[128,1,128]{0,2,1:T(8,128)(2,1)S(1)}, bf16[128,1,128]{0,2,1:T(8,128)(2,1)S(1)}, u32[]{:S(2)}, u32[]{:S(2)}) collective-permute-start(bf16[128,1,128]{0,2,1:T(8,128)(2,1)S(1)} %get-tuple-element.18), channel_id=1, source_target_pairs={{24,0},{32,8},{40,16},{48,24},{56,32},{64,40},{72,48},{80,56},{88,... | collective-permute-start | bytes 98312 | tf_op jit(solution)/shard_map/ppermute | solution.py:18
  221.9 3.2 %collective-permute-start.25 = (bf16[128,1,128]{0,2,1:T(8,128)(2,1)S(1)}, bf16[128,1,128]{0,2,1:T(8,128)(2,1)S(1)}, u32[]{:S(2)}, u32[]{:S(2)}) collective-permute-start(bf16[128,1,128]{0,2,1:T(8,128)(2,1)S(1)} %get-tuple-element.22), channel_id=1, source_target_pairs={{64,0},{72,8},{80,16},{88,24},{96,32},{104,40},{112,48},{120,56},{... | collective-permute-start | bytes 98312 | tf_op jit(solution)/shard_map/ppermute | solution.py:18
  237.6 3.3 %collective-permute-done.19 = bf16[128,1,128]{0,2,1:T(8,128)(2,1)S(1)} collective-permute-done((bf16[128,1,128]{0,2,1:T(8,128)(2,1)S(1)}, bf16[128,1,128]{0,2,1:T(8,128)(2,1)S(1)}, u32[]{:S(2)}, u32[]{:S(2)}) %collective-permute-start.19) | collective-permute-done | bytes 32800 | tf_op jit(solution)/shard_map/ppermute | solution.py:18
  242.8 5.3 %all-to-all-start.3 = ((bf16[8,16,4096]{2,1,0:T(8,128)(2,1)}), bf16[8,16,4096]{2,1,0:T(8,128)(2,1)S(1)}, u32[]{:S(2)}, u32[]{:S(2)}) async-start(bf16[8,16,4096]{2,1,0:T(8,128)(2,1)} %bitcast.123), calls=%async_computation.3 | async-start | bytes 2097152 | tf_op jit(solution)/shard_map/all_to_all | solution.py:44
  248.3 14.7 %all-to-all-done.3 = bf16[8,16,4096]{2,1,0:T(8,128)(2,1)S(1)} async-done(((bf16[8,16,4096]{2,1,0:T(8,128)(2,1)}), bf16[8,16,4096]{2,1,0:T(8,128)(2,1)S(1)}, u32[]{:S(2)}, u32[]{:S(2)}) %all-to-all-start.3) | async-done | bytes 1048608 | tf_op jit(solution)/shard_map/all_to_all | solution.py:44
  263.5 19.4 %all_to_all.31 = bf16[8,16,4096]{2,1,0:T(8,128)(2,1)S(1)} all-to-all(bf16[8,16,4096]{2,1,0:T(8,128)(2,1)S(1)} %broadcast_in_dim.18), channel_id=1, replica_groups=mesh['group'=4,'seq'=16,'mp'=8] {'mp'}, dimensions={0} | all-to-all | bytes 2097152 | tf_op jit(solution)/shard_map/all_to_all | solution.py:23
  282.9 4.8 %convolution_convert_fusion.1 = bf16[128,2560]{1,0:T(8,128)(2,1)S(1)} fusion(bf16[2560,320]{1,0:T(8,128)(2,1)} %bitcast.120, bf16[128,4096]{1,0:T(8,128)(2,1)S(1)} %bitcast.122, bf16[320,4096]{1,0:T(8,128)(2,1)} %all-gather.3.cloned.1.call-done, f32[128,320]{0,1:T(8,128)S(1)} %copy-done.5), kind=kOutput, calls=%fused_computation.7 | convolution fusion | flops 545996800 | bytes 6127616 | tf_op jit(solution)/shard_map/th,fh->tf/dot_general | solution.py:196
  288.9 3.5 %all-to-all-start.5 = ((bf16[8,64,640]{2,1,0:T(8,128)(2,1)}), bf16[8,64,640]{2,1,0:T(8,128)(2,1)S(1)}, u32[]{:S(2)}, u32[]{:S(2)}) async-start(bf16[8,64,640]{2,1,0:T(8,128)(2,1)} %convert_element_type.206), calls=%async_computation.5 | async-start | bytes 1310720 | tf_op jit(solution)/shard_map/all_to_all | solution.py:44
  292.6 9.3 %all-to-all-done.5 = bf16[8,64,640]{2,1,0:T(8,128)(2,1)S(1)} async-done(((bf16[8,64,640]{2,1,0:T(8,128)(2,1)}), bf16[8,64,640]{2,1,0:T(8,128)(2,1)S(1)}, u32[]{:S(2)}, u32[]{:S(2)}) %all-to-all-start.5) | async-done | bytes 655392 | tf_op jit(solution)/shard_map/all_to_all | solution.py:44
  (133 shorter events, 71.1 us)
Async XLA Ops:
  6.5 77.4 %all-gather.3.cloned.1.call-start = ((), (), s32[]{:S(2)}) async-start(), calls=%async_computation.6 | async-start | bytes 2785280 | tf_op jit(solution)/shard_map/all_gather | solution.py:92
  7.3 128.8 %all-gather.5.cloned.1.call-start = ((), (), s32[]{:S(2)}) async-start(), calls=%async_computation.7 | async-start | bytes 6684672 | tf_op jit(solution)/shard_map/all_gather | solution.py:53
  12.3 63.2 %all-to-all-start = ((bf16[16,4,40,320]{3,2,1,0:T(8,128)(2,1)}), bf16[16,4,40,320]{3,2,1,0:T(8,128)(2,1)S(1)}, u32[]{:S(2)}, u32[]{:S(2)}) async-start(bf16[16,4,40,320]{3,2,1,0:T(8,128)(2,1)} %broadcast_in_dim.14), calls=%async_computation | async-start | bytes 3932160 | tf_op jit(solution)/shard_map/all_to_all | solution.py:23
  109.1 17.6 %all-to-all-start.2 = ((bf16[8,16,4096]{2,1,0:T(8,128)(2,1)}), bf16[8,16,4096]{2,1,0:T(8,128)(2,1)S(1)}, u32[]{:S(2)}, u32[]{:S(2)}) async-start(bf16[8,16,4096]{2,1,0:T(8,128)(2,1)} %broadcast_in_dim.15), calls=%async_computation.2 | async-start | bytes 2097152 | tf_op jit(solution)/shard_map/all_to_all | solution.py:23
  138.1 57.3 %collective-permute-start.8 = (bf16[128,256]{1,0:T(8,128)(2,1)S(1)}, bf16[128,256]{1,0:T(8,128)(2,1)S(1)}, u32[]{:S(2)}, u32[]{:S(2)}) collective-permute-start(bf16[128,256]{1,0:T(8,128)(2,1)S(1)} %fusion.37), channel_id=1, source_target_pairs={{0,8},{8,16},{16,24},{24,32},{32,40},{40,48},{48,56},{56,64},{64,7... | collective-permute-start | bytes 196616 | tf_op jit(solution)/shard_map/ppermute | solution.py:18
  140.4 55.0 %collective-permute-start.7 = (bf16[128,256]{1,0:T(8,128)(2,1)S(1)}, bf16[128,256]{1,0:T(8,128)(2,1)S(1)}, u32[]{:S(2)}, u32[]{:S(2)}) collective-permute-start(bf16[128,256]{1,0:T(8,128)(2,1)S(1)} %fusion.37), channel_id=1, source_target_pairs={{0,16},{8,24},{16,32},{24,40},{32,48},{40,56},{48,64},{56,72},{64,... | collective-permute-start | bytes 196616 | tf_op jit(solution)/shard_map/ppermute | solution.py:18
  143.7 51.7 %collective-permute-start.6 = (bf16[128,256]{1,0:T(8,128)(2,1)S(1)}, bf16[128,256]{1,0:T(8,128)(2,1)S(1)}, u32[]{:S(2)}, u32[]{:S(2)}) collective-permute-start(bf16[128,256]{1,0:T(8,128)(2,1)S(1)} %fusion.37), channel_id=1, source_target_pairs={{0,24},{8,32},{16,40},{24,48},{32,56},{40,64},{48,72},{56,80},{64,... | collective-permute-start | bytes 196616 | tf_op jit(solution)/shard_map/ppermute | solution.py:18
  145.6 49.8 %collective-permute-start.5 = (bf16[128,256]{1,0:T(8,128)(2,1)S(1)}, bf16[128,256]{1,0:T(8,128)(2,1)S(1)}, u32[]{:S(2)}, u32[]{:S(2)}) collective-permute-start(bf16[128,256]{1,0:T(8,128)(2,1)S(1)} %fusion.37), channel_id=1, source_target_pairs={{0,32},{8,40},{16,48},{24,56},{32,64},{40,72},{48,80},{56,88},{64,... | collective-permute-start | bytes 196616 | tf_op jit(solution)/shard_map/ppermute | solution.py:18
  155.9 10.1 %collective-permute-start.1 = (bf16[128,256]{1,0:T(8,128)(2,1)S(1)}, bf16[128,256]{1,0:T(8,128)(2,1)S(1)}, u32[]{:S(2)}, u32[]{:S(2)}) collective-permute-start(bf16[128,256]{1,0:T(8,128)(2,1)S(1)} %fusion.37), channel_id=1, source_target_pairs={{0,64},{8,72},{16,80},{24,88},{32,96},{40,104},{48,112},{56,120},{... | collective-permute-start | bytes 196616 | tf_op jit(solution)/shard_map/ppermute | solution.py:18
  175.5 11.1 %collective-permute-start.3 = (bf16[128,256]{1,0:T(8,128)(2,1)S(1)}, bf16[128,256]{1,0:T(8,128)(2,1)S(1)}, u32[]{:S(2)}, u32[]{:S(2)}) collective-permute-start(bf16[128,256]{1,0:T(8,128)(2,1)S(1)} %fusion.37), channel_id=1, source_target_pairs={{0,48},{8,56},{16,64},{24,72},{32,80},{40,88},{48,96},{56,104},{64... | collective-permute-start | bytes 196616 | tf_op jit(solution)/shard_map/ppermute | solution.py:18
  199.2 9.7 %collective-permute-start.9 = (bf16[128,1,128]{0,2,1:T(8,128)(2,1)S(1)}, bf16[128,1,128]{0,2,1:T(8,128)(2,1)S(1)}, u32[]{:S(2)}, u32[]{:S(2)}) collective-permute-start(bf16[128,1,128]{0,2,1:T(8,128)(2,1)S(1)} %get-tuple-element.11), channel_id=1, source_target_pairs={{8,0},{16,8},{24,16},{32,24},{40,32},{48,40},{56,48},{64,56},{72,6... | collective-permute-start | bytes 98312 | tf_op jit(solution)/shard_map/ppermute | solution.py:18
  204.3 11.7 %collective-permute-start.15 = (bf16[128,1,128]{0,2,1:T(8,128)(2,1)S(1)}, bf16[128,1,128]{0,2,1:T(8,128)(2,1)S(1)}, u32[]{:S(2)}, u32[]{:S(2)}) collective-permute-start(bf16[128,1,128]{0,2,1:T(8,128)(2,1)S(1)} %get-tuple-element.14), channel_id=1, source_target_pairs={{56,0},{64,8},{72,16},{80,24},{88,32},{96,40},{104,48},{112,56},{1... | collective-permute-start | bytes 98312 | tf_op jit(solution)/shard_map/ppermute | solution.py:18
  207.0 11.3 %collective-permute-start.14 = (bf16[128,1,128]{0,2,1:T(8,128)(2,1)S(1)}, bf16[128,1,128]{0,2,1:T(8,128)(2,1)S(1)}, u32[]{:S(2)}, u32[]{:S(2)}) collective-permute-start(bf16[128,1,128]{0,2,1:T(8,128)(2,1)S(1)} %get-tuple-element.15), channel_id=1, source_target_pairs={{48,0},{56,8},{64,16},{72,24},{80,32},{88,40},{96,48},{104,56},{11... | collective-permute-start | bytes 98312 | tf_op jit(solution)/shard_map/ppermute | solution.py:18
  208.9 11.6 %collective-permute-start.13 = (bf16[128,1,128]{0,2,1:T(8,128)(2,1)S(1)}, bf16[128,1,128]{0,2,1:T(8,128)(2,1)S(1)}, u32[]{:S(2)}, u32[]{:S(2)}) collective-permute-start(bf16[128,1,128]{0,2,1:T(8,128)(2,1)S(1)} %get-tuple-element.16), channel_id=1, source_target_pairs={{40,0},{48,8},{56,16},{64,24},{72,32},{80,40},{88,48},{96,56},{104... | collective-permute-start | bytes 98312 | tf_op jit(solution)/shard_map/ppermute | solution.py:18
  210.2 11.6 %collective-permute-start.12 = (bf16[128,1,128]{0,2,1:T(8,128)(2,1)S(1)}, bf16[128,1,128]{0,2,1:T(8,128)(2,1)S(1)}, u32[]{:S(2)}, u32[]{:S(2)}) collective-permute-start(bf16[128,1,128]{0,2,1:T(8,128)(2,1)S(1)} %get-tuple-element.17), channel_id=1, source_target_pairs={{32,0},{40,8},{48,16},{56,24},{64,32},{72,40},{80,48},{88,56},{96,... | collective-permute-start | bytes 98312 | tf_op jit(solution)/shard_map/ppermute | solution.py:18
  211.5 13.5 %collective-permute-start.11 = (bf16[128,1,128]{0,2,1:T(8,128)(2,1)S(1)}, bf16[128,1,128]{0,2,1:T(8,128)(2,1)S(1)}, u32[]{:S(2)}, u32[]{:S(2)}) collective-permute-start(bf16[128,1,128]{0,2,1:T(8,128)(2,1)S(1)} %get-tuple-element.18), channel_id=1, source_target_pairs={{24,0},{32,8},{40,16},{48,24},{56,32},{64,40},{72,48},{80,56},{88,... | collective-permute-start | bytes 98312 | tf_op jit(solution)/shard_map/ppermute | solution.py:18
  215.9 12.1 %collective-permute-start.10 = (bf16[128,1,128]{0,2,1:T(8,128)(2,1)S(1)}, bf16[128,1,128]{0,2,1:T(8,128)(2,1)S(1)}, u32[]{:S(2)}, u32[]{:S(2)}) collective-permute-start(bf16[128,1,128]{0,2,1:T(8,128)(2,1)S(1)} %get-tuple-element.19), channel_id=1, source_target_pairs={{16,0},{24,8},{32,16},{40,24},{48,32},{56,40},{64,48},{72,56},{80,... | collective-permute-start | bytes 98312 | tf_op jit(solution)/shard_map/ppermute | solution.py:18
  218.4 11.1 %collective-permute-start.18 = (bf16[128,1,128]{0,2,1:T(8,128)(2,1)S(1)}, bf16[128,1,128]{0,2,1:T(8,128)(2,1)S(1)}, u32[]{:S(2)}, u32[]{:S(2)}) collective-permute-start(bf16[128,1,128]{0,2,1:T(8,128)(2,1)S(1)} %get-tuple-element.20), channel_id=1, source_target_pairs={{8,0},{16,8},{24,16},{32,24},{40,32},{48,40},{56,48},{64,56},{72,6... | collective-permute-start | bytes 98312 | tf_op jit(solution)/shard_map/ppermute | solution.py:18
  220.6 10.2 %collective-permute-start.26 = (bf16[128,1,128]{0,2,1:T(8,128)(2,1)S(1)}, bf16[128,1,128]{0,2,1:T(8,128)(2,1)S(1)}, u32[]{:S(2)}, u32[]{:S(2)}) collective-permute-start(bf16[128,1,128]{0,2,1:T(8,128)(2,1)S(1)} %get-tuple-element.21), channel_id=1, source_target_pairs={{72,0},{80,8},{88,16},{96,24},{104,32},{112,40},{120,48},{73,1},{8... | collective-permute-start | bytes 98312 | tf_op jit(solution)/shard_map/ppermute | solution.py:18
  221.9 10.2 %collective-permute-start.25 = (bf16[128,1,128]{0,2,1:T(8,128)(2,1)S(1)}, bf16[128,1,128]{0,2,1:T(8,128)(2,1)S(1)}, u32[]{:S(2)}, u32[]{:S(2)}) collective-permute-start(bf16[128,1,128]{0,2,1:T(8,128)(2,1)S(1)} %get-tuple-element.22), channel_id=1, source_target_pairs={{64,0},{72,8},{80,16},{88,24},{96,32},{104,40},{112,48},{120,56},{... | collective-permute-start | bytes 98312 | tf_op jit(solution)/shard_map/ppermute | solution.py:18
  225.1 9.9 %collective-permute-start.24 = (bf16[128,1,128]{0,2,1:T(8,128)(2,1)S(1)}, bf16[128,1,128]{0,2,1:T(8,128)(2,1)S(1)}, u32[]{:S(2)}, u32[]{:S(2)}) collective-permute-start(bf16[128,1,128]{0,2,1:T(8,128)(2,1)S(1)} %get-tuple-element.23), channel_id=1, source_target_pairs={{56,0},{64,8},{72,16},{80,24},{88,32},{96,40},{104,48},{112,56},{1... | collective-permute-start | bytes 98312 | tf_op jit(solution)/shard_map/ppermute | solution.py:18
  228.0 9.6 %collective-permute-start.23 = (bf16[128,1,128]{0,2,1:T(8,128)(2,1)S(1)}, bf16[128,1,128]{0,2,1:T(8,128)(2,1)S(1)}, u32[]{:S(2)}, u32[]{:S(2)}) collective-permute-start(bf16[128,1,128]{0,2,1:T(8,128)(2,1)S(1)} %get-tuple-element.24), channel_id=1, source_target_pairs={{48,0},{56,8},{64,16},{72,24},{80,32},{88,40},{96,48},{104,56},{11... | collective-permute-start | bytes 98312 | tf_op jit(solution)/shard_map/ppermute | solution.py:18
  242.8 20.2 %all-to-all-start.3 = ((bf16[8,16,4096]{2,1,0:T(8,128)(2,1)}), bf16[8,16,4096]{2,1,0:T(8,128)(2,1)S(1)}, u32[]{:S(2)}, u32[]{:S(2)}) async-start(bf16[8,16,4096]{2,1,0:T(8,128)(2,1)} %bitcast.123), calls=%async_computation.3 | async-start | bytes 2097152 | tf_op jit(solution)/shard_map/all_to_all | solution.py:44
  288.9 12.9 %all-to-all-start.5 = ((bf16[8,64,640]{2,1,0:T(8,128)(2,1)}), bf16[8,64,640]{2,1,0:T(8,128)(2,1)S(1)}, u32[]{:S(2)}, u32[]{:S(2)}) async-start(bf16[8,64,640]{2,1,0:T(8,128)(2,1)} %convert_element_type.206), calls=%async_computation.5 | async-start | bytes 1310720 | tf_op jit(solution)/shard_map/all_to_all | solution.py:44
  (20 other events, 265.1 us)
Sparse Core Ops, SparseCore 0:
  9.4 74.4 all-gather.2
  86.0 49.9 all-gather.4

commit v2 on v0

v2 whole, which is shorter than its diff:
```python
import functools

import jax
import jax.numpy as jnp
from jax import lax
from jax.experimental import pallas as pl
from jax.experimental.pallas import tpu as pltpu
from jax.sharding import PartitionSpec as P

HEAD = 128
EPSILON = 1e-06
NEGATIVE = 1e30
BF = jnp.bfloat16
F32 = jnp.float32
N_BLOCKS = 10


def gelu_grad(inputs):
    normal_cdf = 0.5 * (1.0 + lax.erf(inputs * 0.7071067811865476))
    normal_pdf = jnp.exp(-0.5 * inputs * inputs) * 0.3989422804014327
    return normal_cdf + inputs * normal_pdf


def dot(a, b):
    return jnp.dot(a, b, preferred_element_type=F32)


def dot_nt(a, b):
    return lax.dot_general(a, b, (((1,), (1,)), ((), ())), preferred_element_type=F32)


def dot_tn(a, b):
    return lax.dot_general(a, b, (((0,), (0,)), ((), ())), preferred_element_type=F32)


def rows(start, count):
    return pl.ds(pl.multiple_of(start, count), count)


def kernel(
    n_seq,
    n_mp,
    patches,
    w1,
    w2,
    wq,
    wkv,
    attn_grad,
    sample_ids,
    out,
    w1g,
    w1n,
    w2g,
    wqg,
    wkvg,
    normed,
    scale,
    hidden_pre,
    hidden,
    part,
    recv,
    merged,
    tok_bf,
    query,
    keys,
    values,
    bias,
    dkeys,
    dvalues,
    ret_send,
    ret_recv,
    chain_send,
    chain_recv,
    blk_send,
    blk_recv,
    dquery,
    grads_kv,
    dn_acc,
    part2,
    recv2,
    dmerged,
    part3,
    recv3,
    out_f32,
    w_send,
    w_recv,
    w_sib,
    rs_send,
    rs_recv,
    kv_send,
    kv_recv,
    ret_ssem,
    ret_rsem,
):
    i = lax.axis_index("seq")
    m = lax.axis_index("mp")
    core = i % 2
    n_chip = n_seq // 2
    sib = i + 1 - 2 * core
    up = (i + 2) % n_seq
    down = (i + n_seq - 2) % n_seq
    far = (i + 9 * core + (n_seq - 9) * (1 - core)) % n_seq
    tok = attn_grad.shape[0]
    share = tok // n_mp
    feat = patches.shape[1]
    fs = feat // n_seq
    dblk = wq.shape[0]

    def seq_copy(src, dst, ssem, rsem, target):
        return pltpu.make_async_remote_copy(
            src_ref=src,
            dst_ref=dst,
            send_sem=ssem,
            recv_sem=rsem,
            device_id={"seq": target},
            device_id_type=pl.DeviceIdType.MESH,
        )

    barrier = pltpu.get_barrier_semaphore()
    for target in (up, down, sib, far):
        pl.semaphore_signal(
            barrier, inc=1, device_id={"seq": target}, device_id_type=pl.DeviceIdType.MESH
        )
    for o in range(1, n_mp):
        pl.semaphore_signal(
            barrier,
            inc=1,
            device_id={"mp": (m + o) % n_mp},
            device_id_type=pl.DeviceIdType.MESH,
        )
    pl.semaphore_wait(barrier, 4 + n_mp - 1)

    sends = []

    own_w = (w1, w2, wq, wkv)
    all_w = (w1g, w2g, wqg, wkvg)
    lead = tuple(None if a.shape[0] == n_seq else o.shape[0] for o, a in zip(own_w, all_w))

    def slot(p, s):
        if lead[p] is None:
            return all_w[p].at[s]
        return all_w[p].at[rows(s * lead[p], lead[p])]

    source = [(i + n_seq - 2 * d) % n_seq for d in (1, 2, 3)]
    source += [(i + 2 * d) % n_seq for d in (1, 2, 3)]
    source += [(i + n_seq // 2) % n_seq]
    sib_source = [(s + 1 - 2 * core) for s in source] + [sib]
    far_up = 1 - core
    turn = (i + 2 * far_up + (n_seq - 2) * (1 - far_up)) % n_seq
    turn_source = (i + (n_seq - 6) * far_up + 6 * (1 - far_up)) % n_seq

    def ring(p, k, s, target):
        return seq_copy(slot(p, s), slot(p, s), w_send.at[p, k], w_recv.at[p, k], target)

    def to_sib(p, k, s):
        return seq_copy(slot(p, s), slot(p, s), w_send.at[p, 7 + k], w_sib.at[p, k], sib)

    def arrived(p, k):
        ring(p, k, source[k], sib).wait_recv()

    def start(copy):
        copy.start()
        sends.append(copy)

    def hop(p, h):
        if h == 1:
            src = own_w[p]
            start(seq_copy(src, slot(p, i), w_send.at[p, 0], w_recv.at[p, 0], up))
            start(seq_copy(src, slot(p, i), w_send.at[p, 3], w_recv.at[p, 3], down))
            start(seq_copy(src, slot(p, i), w_send.at[p, 14], w_sib.at[p, 7], sib))
        elif h <= 3:
            for first, target in ((0, up), (3, down)):
                k = first + h - 2
                arrived(p, k)
                start(ring(p, k + 1, source[k], target))
                start(to_sib(p, k, source[k]))
        elif h == 4:
            for k in (2, 5):
                arrived(p, k)
            start(ring(p, 6, turn_source, turn))
            for k in (2, 5):
                start(to_sib(p, k, source[k]))
        else:
            arrived(p, 6)
            start(to_sib(p, 6, source[6]))

    def gathered(p):
        for k in range(8):
            s = sib_source[k]
            seq_copy(slot(p, s), slot(p, s), w_send.at[p, 7 + k], w_sib.at[p, k], sib).wait_recv()

    def own_slot(p):
        if lead[p] is None:
            all_w[p][i] = own_w[p][...]
        else:
            all_w[p][rows(i * lead[p], lead[p]), :] = own_w[p][...]

    def scatter(step, src, dst):
        for o in range(1, n_mp):
            peer = (m + o) % n_mp
            copy = pltpu.make_async_remote_copy(
                src_ref=src.at[rows(peer * share, share)],
                dst_ref=dst.at[n_mp - o],
                send_sem=rs_send.at[step, o],
                recv_sem=rs_recv.at[step, n_mp - o],
                device_id={"mp": peer},
                device_id_type=pl.DeviceIdType.MESH,
            )
            start(copy)

    def scattered(step, src, dst):
        for o in range(1, n_mp):
            pltpu.make_async_remote_copy(
                src_ref=src.at[rows(m * share, share)],
                dst_ref=dst.at[o],
                send_sem=rs_send.at[step, o],
                recv_sem=rs_recv.at[step, o],
                device_id={"mp": (m + o) % n_mp},
                device_id_type=pl.DeviceIdType.MESH,
            ).wait_recv()

    def spread(step, buf):
        mine = buf.at[rows(m * share, share)]
        for o in range(1, n_mp):
            copy = pltpu.make_async_remote_copy(
                src_ref=mine,
                dst_ref=mine,
                send_sem=rs_send.at[step, o],
                recv_sem=rs_recv.at[step, n_mp - o],
                device_id={"mp": (m + o) % n_mp},
                device_id_type=pl.DeviceIdType.MESH,
            )
            start(copy)

    def spread_done(step, buf):
        for o in range(1, n_mp):
            theirs = buf.at[rows(((m + o) % n_mp) * share, share)]
            pltpu.make_async_remote_copy(
                src_ref=theirs,
                dst_ref=theirs,
                send_sem=rs_send.at[step, o],
                recv_sem=rs_recv.at[step, o],
                device_id={"mp": (m + o) % n_mp},
                device_id_type=pl.DeviceIdType.MESH,
            ).wait_recv()

    def normed_rows(at):
        return jnp.concatenate([normed[j, at, :] for j in range(feat // 128)], 1)

    hop(0, 1)
    hop(1, 1)
    for p in range(4):
        own_slot(p)

    chunk = patches.shape[0] // 4

    @pl.loop(0, 4)
    def _(c):
        at = rows(c * chunk, chunk)
        x = patches[at, :].astype(F32)
        mean = jnp.mean(x, -1, keepdims=True)
        r = lax.rsqrt(jnp.mean(x * x, -1, keepdims=True) - mean * mean + EPSILON)
        x = (x - mean) * r
        for j in range(feat // 128):
            normed[j, at, :] = x[:, j * 128 : (j + 1) * 128]
        scale[at, :] = jnp.broadcast_to(r, (chunk, 128))

    blk_src = [i, (i + (n_seq - 9) * (1 - core) + (n_seq - 1) * core) % n_seq]
    blk_src += [(i + n_seq - 2 * d) % n_seq for d in (1, 2, 3, 4)]
    blk_src += [(i + n_seq - 2 * d + 1 - 2 * core) % n_seq for d in (1, 2, 3, 4)]
    own_ids = sample_ids[0:1, rows(i * tok, tok)]
    q_ids = jnp.transpose(jnp.broadcast_to(own_ids, (tok, tok)))
    row = lax.broadcasted_iota(jnp.int32, (tok, tok), 0)
    lane = lax.broadcasted_iota(jnp.int32, (tok, tok), 1)
    for b in range(N_BLOCKS):
        s = blk_src[b]
        ids = jnp.broadcast_to(sample_ids[0:1, rows(s * tok, tok)], (tok, tok))
        allowed = (ids == q_ids) & (s * tok + lane <= i * tok + row)
        bias[:, b * tok : (b + 1) * tok] = jnp.where(allowed, 0.0, -NEGATIVE)

    hop(0, 2)
    hop(1, 2)
    hop(0, 3)
    hop(1, 3)
    hop(0, 4)
    hop(1, 4)
    hop(0, 5)
    gathered(0)

    for t in range(n_seq // 2):
        a = w1g[2 * t].astype(F32)
        b = w1g[2 * t + 1].astype(F32)
        for p in range(4):
            piece = jnp.concatenate([a[p * fs : (p + 1) * fs], b[p * fs : (p + 1) * fs]], 0)
            w1n[p * feat + 2 * fs * t : p * feat + 2 * fs * (t + 1), :] = piece.astype(BF)

    acc = jnp.zeros((tok, w1.shape[1]), F32)
    for p in range(4):
        x = normed_rows(pl.ds(p, tok, stride=4)).astype(BF)
        acc = acc + dot(x, w1n[p * feat : (p + 1) * feat, :])
    hidden_pre[...] = acc
    hidden[...] = (acc * 0.5 * (1.0 + lax.erf(acc * 0.7071067811865476))).astype(BF)

    hop(1, 5)
    hop(2, 1)
    hop(3, 1)
    gathered(1)
    for s in range(n_seq):
        part[:, s * dblk : (s + 1) * dblk] = dot(hidden[...], w2g[s]).astype(BF)
    scatter(0, part, recv)
    hop(2, 2)
    hop(3, 2)
    scattered(0, part, recv)

    width = part.shape[1]
    n_cols = width // 512 if width % 512 == 0 else 1
    cols = width // n_cols

    @pl.loop(0, n_cols)
    def _(c):
        at = rows(c * cols, cols)
        total = part[rows(m * share, share), at].astype(F32)
        for o in range(1, n_mp):
            total = total + recv[o, :, at].astype(F32)
        merged[rows(m * share, share), at] = total.astype(BF)

    spread(1, merged)
    hop(2, 3)
    hop(3, 3)
    spread_done(1, merged)

    @pl.loop(0, tok // 16)
    def _(c):
        at = rows(c * 16, 16)
        x = merged[at, :].astype(F32)
        r = lax.rsqrt(jnp.mean(x * x, -1, keepdims=True) + EPSILON)
        tok_bf[at, :] = (x * r).astype(BF)

    hop(2, 4)
    hop(3, 4)
    hop(2, 5)
    hop(3, 5)
    gathered(3)
    kv = dot(tok_bf[...], wkvg[...])
    keys[0:tok, :] = kv[:, :HEAD].astype(BF)
    values[0:tok, :] = kv[:, HEAD:].astype(BF)

    near = core * ((i + 9) % n_seq) + (1 - core) * sib

    def kv_copy(which, src_block, dst_block, sem, target):
        buf = (keys, values)[which]
        return seq_copy(
            buf.at[src_block * tok : (src_block + 1) * tok],
            buf.at[dst_block * tok : (dst_block + 1) * tok],
            kv_send.at[which, sem],
            kv_recv.at[which, dst_block],
            target,
        )

    for which in (0, 1):
        start(kv_copy(which, 0, 2, 0, up))
        start(kv_copy(which, 0, 1, 1, near))
    gathered(2)
    qw = wq.shape[1]
    per_kv = qw // HEAD
    for h in range(per_kv):
        at = slice(h * HEAD, (h + 1) * HEAD)
        query[h * tok : (h + 1) * tok, :] = dot(tok_bf[...], wqg[:, at]).astype(BF)
    for d in (1, 2, 3, 4):
        for which in (0, 1):
            kv_copy(which, 1 + d, 1 + d, 0, up).wait_recv()
            if d < 4:
                start(kv_copy(which, 1 + d, 2 + d, 1 + d, up))
            start(kv_copy(which, 1 + d, 5 + d, 4 + d, sib))
    for which in (0, 1):
        for b in (1, 6, 7, 8, 9):
            kv_copy(which, b, b, 0, sib).wait_recv()

    score_scale = HEAD ** (-0.5)
    dkeys[...] = jnp.zeros_like(dkeys)
    dvalues[...] = jnp.zeros_like(dvalues)

    for h in range(per_kv):
        at = slice(h * HEAD, (h + 1) * HEAD)
        q = query[h * tok : (h + 1) * tok, :]
        g = attn_grad[:, at]
        s = dot_nt(q, keys[...]) * score_scale + bias[...]
        e = jnp.exp(s - jnp.max(s, -1, keepdims=True))
        soft = e / jnp.sum(e, -1, keepdims=True)
        soft_bf = soft.astype(BF)
        attended = dot(soft_bf, values[...])
        delta = jnp.sum(g.astype(F32) * attended, -1, keepdims=True)
        dprob = dot_nt(g, values[...])
        ds = (soft * (dprob - delta)).astype(BF)
        dquery[:, at] = (dot(ds, keys[...]) * score_scale).astype(BF)
        dkeys[...] += dot_tn(ds, q) * score_scale
        dvalues[...] += dot_tn(soft_bf, g)

    grads = (dkeys, dvalues)
    back = core * sib + (1 - core) * far

    def ret_copy(which, target):
        return seq_copy(
            ret_send.at[which], ret_recv.at[which], ret_ssem.at[which, 0], ret_rsem.at[which, 0], target
        )

    def blk_copy(which, target):
        return seq_copy(
            blk_send.at[which], blk_recv.at[which], ret_ssem.at[which, 1], ret_rsem.at[which, 1], target
        )

    def chain_copy(which, d, target):
        return seq_copy(
            chain_send.at[which, d - 1],
            chain_recv.at[which, d - 1],
            ret_ssem.at[which, 1 + d],
            ret_rsem.at[which, 1 + d],
            target,
        )

    for which in (0, 1):
        ret_send[which] = grads[which][6 * tok :, :].astype(BF)
        start(ret_copy(which, sib))
    for which in (0, 1):
        blk_send[which] = grads[which][tok : 2 * tok, :].astype(BF)
        start(blk_copy(which, back))

    def chain_step(which, d):
        if d == 4:
            ret_copy(which, sib).wait_recv()
        total = grads[which][(1 + d) * tok : (2 + d) * tok, :]
        total = total + ret_recv[which, (d - 1) * tok : d * tok, :].astype(F32)
        if d < 4:
            chain_copy(which, d + 1, down).wait_recv()
            total = total + chain_recv[which, d].astype(F32)
        chain_send[which, d - 1] = total.astype(BF)
        start(chain_copy(which, d, down))

    for which in (0, 1):
        chain_step(which, 4)
    for quarter in range(4):
        for s in range(quarter * n_seq // 4, (quarter + 1) * n_seq // 4):
            at = slice(s * dblk, (s + 1) * dblk)
            dn_acc[:, at] = dot_nt(dquery[...], wqg[at, :])
        if quarter < 3:
            for which in (0, 1):
                chain_step(which, 3 - quarter)
    for which in (0, 1):
        blk_copy(which, sib).wait_recv()
        chain_copy(which, 1, down).wait_recv()
        total = grads[which][0:tok, :] + blk_recv[which].astype(F32) + chain_recv[which, 0].astype(F32)
        grads_kv[:, which * HEAD : (which + 1) * HEAD] = total.astype(BF)

    for s in range(n_seq):
        at = slice(s * dblk, (s + 1) * dblk)
        part2[:, at] = (dn_acc[:, at] + dot_nt(grads_kv[...], wkvg[at, :])).astype(BF)
    scatter(2, part2, recv2)
    scattered(2, part2, recv2)
    mine = rows(m * share, share)
    x = merged[mine, :].astype(F32)
    r = lax.rsqrt(jnp.mean(x * x, -1, keepdims=True) + EPSILON)
    x = x * r
    dn = part2[mine, :].astype(F32)
    for o in range(1, n_mp):
        dn = dn + recv2[o].astype(F32)
    dmerged[mine, :] = (r * (dn - x * jnp.mean(dn * x, -1, keepdims=True))).astype(BF)
    spread(3, dmerged)
    spread_done(3, dmerged)

    acc = jnp.zeros((tok, w1.shape[1]), F32)
    for s in range(n_seq):
        acc = acc + dot_nt(dmerged[:, s * dblk : (s + 1) * dblk], w2g[s])
    dhidden = (acc * gelu_grad(hidden_pre[...])).astype(BF)
    for p in range(4):
        part3[:, p * feat : (p + 1) * feat] = dot_nt(dhidden, w1n[p * feat : (p + 1) * feat, :]).astype(BF)
    scatter(4, part3, recv3)
    scattered(4, part3, recv3)
    for p in range(4):
        at = slice(p * feat, (p + 1) * feat)
        dx = part3[mine, at].astype(F32)
        for o in range(1, n_mp):
            dx = dx + recv3[o, :, at].astype(F32)
        own = pl.ds(m * (4 * share) + p, share, stride=4)
        nx = normed_rows(own)
        first = jnp.mean(dx, -1, keepdims=True)
        second = jnp.mean(dx * nx, -1, keepdims=True)
        dx = scale[own, :][:, 0:1] * (dx - first - nx * second)
        for j in range(feat // 128):
            out_f32[j, pl.ds(p, share, stride=4), :] = dx[:, j * 128 : (j + 1) * 128]
    for j in range(feat // 128):
        out[:, j * 128 : (j + 1) * 128] = out_f32[j].astype(BF)

    for copy in sends:
        copy.wait_send()


def local(patches, w_merge1, w_merge2, w_query, w_keyval, attn_grad, sample_ids):
    n_seq, n_mp = lax.axis_size("seq"), lax.axis_size("mp")
    w1 = w_merge1.reshape(-1, w_merge1.shape[2])
    wkv = w_keyval.reshape(w_keyval.shape[0], -1)
    tok = attn_grad.shape[0]
    share = tok // n_mp
    feat = patches.shape[1]
    hid = w1.shape[1]
    width = n_seq * w_query.shape[0]
    qw = w_query.shape[1]
    span = N_BLOCKS * tok
    scratch = [
        pltpu.VMEM((n_seq, *w1.shape), BF),
        pltpu.VMEM((4 * feat, hid), BF),
        pltpu.VMEM((n_seq, *w_merge2.shape), BF),
        pltpu.VMEM((width, qw), BF),
        pltpu.VMEM((width, 2 * HEAD), BF),
        pltpu.VMEM((feat // 128, 4 * tok, 128), F32),
        pltpu.VMEM((4 * tok, 128), F32),
        pltpu.VMEM((tok, hid), F32),
        pltpu.VMEM((tok, hid), BF),
        pltpu.VMEM((tok, width), BF),
        pltpu.VMEM((n_mp, share, width), BF),
        pltpu.VMEM((tok, width), BF),
        pltpu.VMEM((tok, width), BF),
        pltpu.VMEM((qw // HEAD * tok, HEAD), BF),
        pltpu.VMEM((span, HEAD), BF),
        pltpu.VMEM((span, HEAD), BF),
        pltpu.VMEM((tok, span), F32),
        pltpu.VMEM((span, HEAD), F32),
        pltpu.VMEM((span, HEAD), F32),
        pltpu.VMEM((2, 4 * tok, HEAD), BF),
        pltpu.VMEM((2, 4 * tok, HEAD), BF),
        pltpu.VMEM((2, 4, tok, HEAD), BF),
        pltpu.VMEM((2, 4, tok, HEAD), BF),
        pltpu.VMEM((2, tok, HEAD), BF),
        pltpu.VMEM((2, tok, HEAD), BF),
        pltpu.VMEM((tok, qw), BF),
        pltpu.VMEM((tok, 2 * HEAD), BF),
        pltpu.VMEM((tok, width), F32),
        pltpu.VMEM((tok, width), BF),
        pltpu.VMEM((n_mp, share, width), BF),
        pltpu.VMEM((tok, width), BF),
        pltpu.VMEM((tok, 4 * feat), BF),
        pltpu.VMEM((n_mp, share, 4 * feat), BF),
        pltpu.VMEM((feat // 128, 4 * share, 128), F32),
        pltpu.SemaphoreType.DMA((4, 15)),
        pltpu.SemaphoreType.DMA((4, 7)),
        pltpu.SemaphoreType.DMA((4, 8)),
        pltpu.SemaphoreType.DMA((5, n_mp)),
        pltpu.SemaphoreType.DMA((5, n_mp)),
        pltpu.SemaphoreType.DMA((2, 9)),
        pltpu.SemaphoreType.DMA((2, N_BLOCKS)),
        pltpu.SemaphoreType.DMA((2, 6)),
        pltpu.SemaphoreType.DMA((2, 6)),
    ]
    vmem = pl.BlockSpec(memory_space=pltpu.VMEM)
    return pl.pallas_call(
        functools.partial(kernel, n_seq, n_mp),
        out_shape=jax.ShapeDtypeStruct((4 * share, feat), BF),
        in_specs=[vmem] * 7,
        out_specs=vmem,
        scratch_shapes=scratch,
        compiler_params=pltpu.CompilerParams(
            collective_id=0, has_side_effects=True, vmem_limit_bytes=56 * 1024 * 1024
        ),
        name="merger",
    )(patches, w1, w_merge2, w_query, wkv, attn_grad, sample_ids)


def solution(mesh):
    in_specs = (
        P(("group", "seq"), None),
        P(None, "seq", "mp"),
        P("mp", "seq"),
        P("seq", "mp"),
        P("seq", None, "mp"),
        P(("group", "seq"), "mp"),
        P("group", None),
    )
    out_specs = P(("group", "seq", "mp"), None)
    return jax.shard_map(local, mesh=mesh, in_specs=in_specs, out_specs=out_specs, check_vma=False)
```

time: 372 us -> 154 us (0.41)
  the two profiles are of different devices: /device:TPU:16 before, /device:TPU:334 now
where the time goes in v2:
time: 154 us
  Pallas kernels  151 us (98%)
  local copies, waits for them, and re-layouts  3.09 us (2%)
    pallas_call x1, Pallas kernels, local(): pl.pallas_call(functools.partial(kernel, n_seq, n_mp), out_shape=jax.Shap...  151 us
    unnamed x2, local copies, waits for them, and re-layouts  3.09 us

profile of v2, /device:TPU:334, one launch (start us, length us, event | category | flops | bytes accessed | tf_op | source)
XLA Modules:
  0.0 153.9 jit_solution(4559761849834367840)
XLA Ops:
  0.0 1.6 %copy.10 = bf16[32,8,2,128]{3,1,2,0:T(8,128)(2,1)} copy(bf16[32,8,2,128]{3,2,1,0:T(2,128)(2,1)} %bitcast.6) | data formatting | bytes 262144
  1.6 150.8 %merger.1 = bf16[64,640]{1,0:T(8,128)(2,1)} custom-call(bf16[512,640]{1,0:T(8,128)(2,1)} %patches.1, bf16[160,320]{1,0:T(8,128)(2,1)} %bitcast.7, bf16[320,256]{1,0:T(8,128)(2,1)} %w2.1, bf16[256,512]{1,0:T(8,128)(2,1)} %wq.1, bf16[256,256]{1,0:T(8,128)(2,1)} %bitcast.5, bf16[128,512]{1,0:T(8,128)(2,1)} %attn_grad.1, s32[1,2048]{1,0:T(1,128)} %sample_ids.1), custom_call_target="tpu_custom_call" | custom-call | tf_op jit(solution)/shard_map/merger/pallas_call | solution.py:554
  152.4 1.5 copy.12

commit v3 on v2

v3 whole, which is shorter than its diff:
```python
import functools

import jax
import jax.numpy as jnp
from jax import lax
from jax.experimental import pallas as pl
from jax.experimental.pallas import tpu as pltpu
from jax.sharding import PartitionSpec as P

HEAD = 128
EPSILON = 1e-06
NEGATIVE = 1e30
BF = jnp.bfloat16
F32 = jnp.float32
N_BLOCKS = 10


def gelu_grad(inputs):
    normal_cdf = 0.5 * (1.0 + lax.erf(inputs * 0.7071067811865476))
    normal_pdf = jnp.exp(-0.5 * inputs * inputs) * 0.3989422804014327
    return normal_cdf + inputs * normal_pdf


def dot(a, b):
    return jnp.dot(a, b, preferred_element_type=F32)


def dot_nt(a, b):
    return lax.dot_general(a, b, (((1,), (1,)), ((), ())), preferred_element_type=F32)


def dot_tn(a, b):
    return lax.dot_general(a, b, (((0,), (0,)), ((), ())), preferred_element_type=F32)


def rows(start, count):
    return pl.ds(pl.multiple_of(start, count), count)


def kernel(
    n_seq,
    n_mp,
    patches_hbm,
    w1_hbm,
    w2_hbm,
    wq_hbm,
    wkv_hbm,
    attn_grad_hbm,
    sample_ids,
    out,
    patches,
    attn_grad,
    wkv_raw,
    wkv_f32,
    w1g,
    w1n,
    w2g,
    wqg,
    wkvg,
    normed,
    scale,
    hidden_pre,
    hidden,
    part,
    recv,
    merged,
    tok_bf,
    query,
    keys,
    values,
    bias,
    dkeys,
    dvalues,
    ret_send,
    ret_recv,
    chain_send,
    chain_recv,
    blk_send,
    blk_recv,
    kv_relay,
    ret_relay,
    dquery,
    grads_kv,
    dn_acc,
    part2,
    recv2,
    dmerged,
    part3,
    recv3,
    out_f32,
    in_sem,
    w_send,
    w_recv,
    w_sib,
    rs_send,
    rs_recv,
    kv_send,
    kv_recv,
    ret_ssem,
    ret_rsem,
):
    i = lax.axis_index("seq")
    m = lax.axis_index("mp")
    core = i % 2
    sib = i + 1 - 2 * core
    up = (i + 2) % n_seq
    down = (i + n_seq - 2) % n_seq
    up2 = (i + 4) % n_seq
    down2 = (i + n_seq - 4) % n_seq
    far = (i + 9 * core + (n_seq - 9) * (1 - core)) % n_seq
    tok, qw = attn_grad.shape
    share = tok // n_mp
    feat = patches.shape[1]
    fs = feat // n_seq
    hid = hidden.shape[1]
    dblk = w2g.shape[2]
    mine = rows(m * share, share)

    def seq_copy(src, dst, ssem, rsem, target):
        return pltpu.make_async_remote_copy(
            src_ref=src,
            dst_ref=dst,
            send_sem=ssem,
            recv_sem=rsem,
            device_id={"seq": target},
            device_id_type=pl.DeviceIdType.MESH,
        )

    barrier = pltpu.get_barrier_semaphore()
    for target in (up, down, up2, down2, sib, far):
        pl.semaphore_signal(
            barrier, inc=1, device_id={"seq": target}, device_id_type=pl.DeviceIdType.MESH
        )
    for o in range(1, n_mp):
        pl.semaphore_signal(
            barrier,
            inc=1,
            device_id={"mp": (m + o) % n_mp},
            device_id_type=pl.DeviceIdType.MESH,
        )

    groups = [(range(0, 3)), (range(3, 5)), (range(5, 7)), (range(7, 8))]
    spans = [slice(2 * g[0] * dblk, (2 * g[-1] + 2) * dblk) for g in groups]

    half2 = w2g.shape[1] // 2
    rq = wqg.shape[0] // n_seq
    W1, W2A, W2B, WKV, WQA, WQB = range(6)

    def slot(p, s):
        if p == W1:
            return w1g.at[s]
        if p in (W2A, W2B):
            return w2g.at[s, pl.ds((p - W2A) * half2, half2)]
        if p == WKV:
            return wkvg.at[rows(s * rq, rq)]
        return wqg.at[pl.ds(pl.multiple_of(s * rq + (p - WQA) * (rq // 2), rq // 2), rq // 2)]

    own_q = wqg.at[rows(core * rq, rq)]
    loads = [
        pltpu.make_async_copy(w1_hbm, w1g.at[core], in_sem.at[0]),
        pltpu.make_async_copy(w2_hbm, w2g.at[core], in_sem.at[1]),
        pltpu.make_async_copy(patches_hbm, patches, in_sem.at[2]),
        pltpu.make_async_copy(wkv_hbm, wkv_raw, in_sem.at[3]),
        pltpu.make_async_copy(wq_hbm, own_q, in_sem.at[4]),
        pltpu.make_async_copy(attn_grad_hbm, attn_grad, in_sem.at[5]),
    ]
    for load in loads:
        load.start()
    loads[0].wait()
    loads[1].wait()
    pl.semaphore_wait(barrier, 6 + n_mp - 1)

    def slots(p, count):
        if p == W1:
            return w1g.at[pl.ds(0, count)]
        if p in (W2A, W2B):
            return w2g.at[pl.ds(0, count), pl.ds((p - W2A) * half2, half2)]
        if p == WKV:
            return wkvg.at[pl.ds(0, count * rq)]
        return wqg.at[pl.ds(0, count * (rq // 2))]

    def ring(p, src_place, dst_place, target):
        seq_copy(
            slot(p, 2 * src_place + core),
            slot(p, 2 * dst_place + core),
            w_send.at[p],
            w_recv.at[p, (dst_place - 1) // 2],
            target,
        ).start()

    def sib_sem(p, place):
        if p == W1:
            return w_sib.at[0]
        if p in (W2A, W2B):
            return w_sib.at[1 + [k for k in range(4) if place in groups[k]][0]]
        return w_sib.at[5 if p == WKV else 6]

    def to_sib(p, place):
        ref = slot(p, 2 * place + core)
        seq_copy(ref, ref, w_send.at[p], sib_sem(p, place), sib).start()

    def arrived(p, step):
        ref = slots(p, 1 if step == 3 else 2)
        seq_copy(ref, ref, w_send.at[p], w_recv.at[p, step], sib).wait_recv()

    turn = core * down + (1 - core) * up

    def hop(p, h):
        if h == 1:
            ring(p, 0, 1, up)
            ring(p, 0, 2, down)
            to_sib(p, 0)
            return
        arrived(p, h - 2)
        if h <= 3:
            ring(p, 2 * h - 3, 2 * h - 1, up)
            ring(p, 2 * h - 2, 2 * h, down)
        elif h == 4:
            ring(p, 5 + core, 7, turn)
        if h <= 4:
            to_sib(p, 2 * h - 3)
            to_sib(p, 2 * h - 2)
        else:
            to_sib(p, 7)

    def gathered(ref, sem):
        seq_copy(ref, ref, w_send.at[0], w_sib.at[sem], sib).wait_recv()

    def mp_copy(step, src, dst, peer):
        return pltpu.make_async_remote_copy(
            src_ref=src,
            dst_ref=dst,
            send_sem=rs_send.at[step],
            recv_sem=rs_recv.at[step],
            device_id={"mp": peer},
            device_id_type=pl.DeviceIdType.MESH,
        )

    mp_sent = []

    def scatter(step, src, dst, at):
        for o in range(1, n_mp):
            peer = (m + o) % n_mp
            theirs = rows(peer * share, share)
            mp_copy(step, src.at[theirs, at], dst.at[n_mp - o, :, at], peer).start()
        mp_sent.append((step, dst.at[pl.ds(1, n_mp - 1), :, at]))

    def scattered(step, dst, at):
        ref = dst.at[pl.ds(1, n_mp - 1), :, at]
        mp_copy(step, ref, ref, (m + 1) % n_mp).wait_recv()

    def total(src, dst, at):
        value = src[mine, at].astype(F32)
        for o in range(1, n_mp):
            value = value + dst[o, :, at].astype(F32)
        return value

    def spread(step, buf, at):
        ref = buf.at[mine, at]
        for o in range(1, n_mp):
            mp_copy(step, ref, ref, (m + o) % n_mp).start()
        mp_sent.append((step, buf.at[pl.ds(0, (n_mp - 1) * share), at]))

    def spread_done(step, buf, at):
        ref = buf.at[pl.ds(0, (n_mp - 1) * share), at]
        mp_copy(step, ref, ref, (m + 1) % n_mp).wait_recv()

    def normed_rows(at):
        return jnp.concatenate([normed[j, at, :] for j in range(feat // 128)], 1)

    hop(W1, 1)
    hop(W2A, 1)

    chunk = patches.shape[0] // 4
    loads[2].wait()

    @pl.loop(0, 4)
    def _(c):
        at = rows(c * chunk, chunk)
        x = patches[at, :].astype(F32)
        mean = jnp.mean(x, -1, keepdims=True)
        r = lax.rsqrt(jnp.mean(x * x, -1, keepdims=True) - mean * mean + EPSILON)
        x = (x - mean) * r
        for j in range(feat // 128):
            normed[j, at, :] = x[:, j * 128 : (j + 1) * 128]
        scale[at, :] = jnp.broadcast_to(r, (chunk, 128))

    loads[3].wait()
    wkv_f32[...] = wkv_raw[...].astype(F32)
    for which in (0, 1):
        shard = wkv_f32[pl.ds(which, rq, stride=2), :].astype(BF)
        wkvg[rows(core * rq, rq), which * HEAD : (which + 1) * HEAD] = shard

    hop(W1, 2)
    hop(W2B, 1)

    blk_src = [i, (i + (n_seq - 9) * (1 - core) + (n_seq - 1) * core) % n_seq]
    blk_src += [(i + n_seq - 2 * d) % n_seq for d in (1, 2, 3, 4)]
    blk_src += [(i + n_seq - 2 * d + 1 - 2 * core) % n_seq for d in (1, 2, 3, 4)]
    own_ids = sample_ids[0:1, rows(i * tok, tok)]
    q_ids = jnp.transpose(jnp.broadcast_to(own_ids, (tok, tok)))
    row = lax.broadcasted_iota(jnp.int32, (tok, tok), 0)
    lane = lax.broadcasted_iota(jnp.int32, (tok, tok), 1)
    for b in range(N_BLOCKS):
        s = blk_src[b]
        ids = jnp.broadcast_to(sample_ids[0:1, rows(s * tok, tok)], (tok, tok))
        allowed = (ids == q_ids) & (s * tok + lane <= i * tok + row)
        bias[:, b * tok : (b + 1) * tok] = jnp.where(allowed, 0.0, -NEGATIVE)

    hop(W1, 3)
    hop(W2A, 2)
    hop(W1, 4)
    hop(W2B, 2)
    hop(W1, 5)
    hop(W2A, 3)
    hop(W2B, 3)
    loads[4].wait()
    hop(WKV, 1)
    gathered(slots(W1, 8), 0)

    for place, step in enumerate((0, -1, 1, -2, 2, -3, 3, 4)):
        chip = (i // 2 + n_seq // 2 + step) % (n_seq // 2)
        a = w1g[2 * place].astype(F32)
        b = w1g[2 * place + 1].astype(F32)
        for p in range(4):
            piece = jnp.concatenate([a[p * fs : (p + 1) * fs], b[p * fs : (p + 1) * fs]], 0)
            at = pl.ds(pl.multiple_of(p * feat + 2 * fs * chip, 2 * fs), 2 * fs)
            w1n[at, :] = piece.astype(BF)

    acc = jnp.zeros((tok, hid), F32)
    for p in range(4):
        x = normed_rows(pl.ds(p, tok, stride=4)).astype(BF)
        acc = acc + dot(x, w1n[p * feat : (p + 1) * feat, :])
    hidden_pre[...] = acc
    hidden[...] = (acc * 0.5 * (1.0 + lax.erf(acc * 0.7071067811865476))).astype(BF)

    def merge_group(g):
        gathered(w2g.at[pl.ds(0, len(groups[g]))], 1 + g)
        for s in range(2 * groups[g][0], 2 * groups[g][-1] + 2):
            part[:, s * dblk : (s + 1) * dblk] = dot(hidden[...], w2g[s]).astype(BF)
        scatter(g, part, recv, spans[g])

    merge_group(0)
    hop(W2A, 4)
    hop(W2B, 4)
    hop(WQA, 1)
    merge_group(1)
    hop(WKV, 2)
    merge_group(2)
    hop(W2A, 5)
    hop(W2B, 5)
    merge_group(3)
    hop(WQA, 2)

    def sum_group(g):
        scattered(g, recv, spans[g])
        for s in range(spans[g].start, spans[g].stop, 2 * dblk):
            at = slice(s, s + 2 * dblk)
            merged[mine, at] = total(part, recv, at).astype(BF)
        spread(4 + g, merged, spans[g])

    sum_group(0)
    hop(WKV, 3)
    sum_group(1)
    hop(WQB, 1)
    sum_group(2)
    hop(WKV, 4)
    sum_group(3)
    hop(WQA, 3)
    hop(WKV, 5)
    hop(WQB, 2)
    hop(WQA, 4)
    for g in range(4):
        spread_done(4 + g, merged, spans[g])

    @pl.loop(0, tok // 16)
    def _(c):
        at = rows(c * 16, 16)
        x = merged[at, :].astype(F32)
        r = lax.rsqrt(jnp.mean(x * x, -1, keepdims=True) + EPSILON)
        tok_bf[at, :] = (x * r).astype(BF)

    hop(WQB, 3)
    gathered(slots(WKV, 8), 5)
    kv = dot(tok_bf[...], wkvg[...])
    keys[0:tok, :] = kv[:, :HEAD].astype(BF)
    values[0:tok, :] = kv[:, HEAD:].astype(BF)

    near = core * ((i + 9) % n_seq) + (1 - core) * sib

    def block(buf, b):
        return buf.at[b * tok : (b + 1) * tok]

    def kv_copy(which, src, dst, arrive, target):
        return seq_copy(src, dst, kv_send.at[which], kv_recv.at[which, arrive], target)

    def kv_step(d):
        for which in (0, 1):
            buf = (keys, values)[which]
            ref = block(buf, 1 + d)
            kv_copy(which, ref, ref, d, sib).wait_recv()
            if d == 1:
                kv_copy(which, ref, block(buf, 4), 3, up2).start()
            kv_copy(which, ref, block(buf, 5 + d), 5, sib).start()

    for which in (0, 1):
        own = block((keys, values)[which], 0)
        kv_copy(which, own, block((keys, values)[which], 2), 1, up).start()
        kv_copy(which, own, kv_relay.at[which], 0, down2).start()
    for which in (0, 1):
        own = block((keys, values)[which], 0)
        kv_copy(which, own, block((keys, values)[which], 3), 2, up2).start()
        kv_copy(which, own, block((keys, values)[which], 1), 5, near).start()
    kv_step(1)
    for which in (0, 1):
        ref = kv_relay.at[which]
        kv_copy(which, ref, ref, 0, sib).wait_recv()
        kv_copy(which, ref, block((keys, values)[which], 5), 4, down2).start()
    hop(WQA, 5)
    hop(WQB, 4)
    kv_step(2)
    kv_step(3)
    kv_step(4)
    hop(WQB, 5)
    gathered(wqg.at[pl.ds(0, 8 * rq)], 6)
    per_kv = qw // HEAD
    for h in range(per_kv):
        at = slice(h * HEAD, (h + 1) * HEAD)
        query[h * tok : (h + 1) * tok, :] = dot(tok_bf[...], wqg[:, at]).astype(BF)
    for which in (0, 1):
        ref = (keys, values)[which].at[0 : 5 * tok]
        kv_copy(which, ref, ref, 5, sib).wait_recv()

    loads[5].wait()
    score_scale = HEAD ** (-0.5)
    dkeys[...] = jnp.zeros_like(dkeys)
    dvalues[...] = jnp.zeros_like(dvalues)

    for h in range(per_kv):
        at = slice(h * HEAD, (h + 1) * HEAD)
        q = query[h * tok : (h + 1) * tok, :]
        g = attn_grad[:, at]
        s = dot_nt(q, keys[...]) * score_scale + bias[...]
        e = jnp.exp(s - jnp.max(s, -1, keepdims=True))
        soft = e / jnp.sum(e, -1, keepdims=True)
        soft_bf = soft.astype(BF)
        attended = dot(soft_bf, values[...])
        delta = jnp.sum(g.astype(F32) * attended, -1, keepdims=True)
        dprob = dot_nt(g, values[...])
        ds = (soft * (dprob - delta)).astype(BF)
        dquery[:, at] = (dot(ds, keys[...]) * score_scale).astype(BF)
        dkeys[...] += dot_tn(ds, q) * score_scale
        dvalues[...] += dot_tn(soft_bf, g)

    grads = (dkeys, dvalues)
    back = core * sib + (1 - core) * far

    def ret_copy(which, src, dst, arrive, target):
        return seq_copy(src, dst, ret_ssem.at[which], ret_rsem.at[which, arrive], target)

    def ret_wait(which, ref, arrive):
        ret_copy(which, ref, ref, arrive, sib).wait_recv()

    for which in (0, 1):
        ret_send[which] = grads[which][6 * tok :, :].astype(BF)
        ret_copy(which, ret_send.at[which], ret_recv.at[which], 0, sib).start()
    for which in (0, 1):
        blk_send[which] = grads[which][tok : 2 * tok, :].astype(BF)
        ret_copy(which, blk_send.at[which], blk_recv.at[which], 1, back).start()

    def chain_step(which, d):
        value = grads[which][(1 + d) * tok : (2 + d) * tok, :]
        value = value + ret_recv[which, (d - 1) * tok : d * tok, :].astype(F32)
        if d == 1:
            ret_wait(which, chain_recv.at[which, 2], 4)
            value = value + chain_recv[which, 2].astype(F32)
        chain_send[which, d - 1] = value.astype(BF)
        src, dst = chain_send.at[which, d - 1], chain_recv.at[which, d - 1]
        if d == 4:
            ret_copy(which, src, ret_relay.at[which], 6, up2).start()
        else:
            ret_copy(which, src, dst, 1 + d, down if d == 1 else down2).start()

    for which in (0, 1):
        ret_wait(which, ret_recv.at[which], 0)
        chain_step(which, 3)
        chain_step(which, 4)
    for which in (0, 1):
        chain_step(which, 2)
    half = n_seq // 2
    for s in range(half):
        at = slice(s * dblk, (s + 1) * dblk)
        dn_acc[:, at] = dot_nt(dquery[...], wqg[at, :])
    for which in (0, 1):
        chain_step(which, 1)
    for which in (0, 1):
        ret_wait(which, ret_relay.at[which], 6)
        ret_copy(which, ret_relay.at[which], chain_recv.at[which, 3], 5, up2).start()
    for s in range(half, n_seq):
        at = slice(s * dblk, (s + 1) * dblk)
        dn_acc[:, at] = dot_nt(dquery[...], wqg[at, :])
    for which in (0, 1):
        ret_wait(which, blk_recv.at[which], 1)
        value = grads[which][0:tok, :] + blk_recv[which].astype(F32)
        for d in (2, 4, 1):
            ret_wait(which, chain_recv.at[which, d - 1], 1 + d)
            value = value + chain_recv[which, d - 1].astype(F32)
        grads_kv[:, which * HEAD : (which + 1) * HEAD] = value.astype(BF)

    for g in range(4):
        for s in range(2 * groups[g][0], 2 * groups[g][-1] + 2):
            at = slice(s * dblk, (s + 1) * dblk)
            part2[:, at] = (dn_acc[:, at] + dot_nt(grads_kv[...], wkvg[at, :])).astype(BF)
        scatter(8 + g, part2, recv2, spans[g])
    for g in range(4):
        scattered(8 + g, recv2, spans[g])
    x = merged[mine, :].astype(F32)
    r = lax.rsqrt(jnp.mean(x * x, -1, keepdims=True) + EPSILON)
    x = x * r
    dn = total(part2, recv2, slice(0, n_seq * dblk))
    dmerged[mine, :] = (r * (dn - x * jnp.mean(dn * x, -1, keepdims=True))).astype(BF)
    for g in range(4):
        spread(12 + g, dmerged, spans[g])
    acc = jnp.zeros((tok, hid), F32)
    for g in range(4):
        spread_done(12 + g, dmerged, spans[g])
        for s in range(2 * groups[g][0], 2 * groups[g][-1] + 2):
            acc = acc + dot_nt(dmerged[:, s * dblk : (s + 1) * dblk], w2g[s])
    dhidden = (acc * gelu_grad(hidden_pre[...])).astype(BF)
    pieces = [slice(p * feat, (p + 1) * feat) for p in range(4)]
    for p in range(4):
        part3[:, pieces[p]] = dot_nt(dhidden, w1n[pieces[p], :]).astype(BF)
        scatter(16 + p, part3, recv3, pieces[p])
    for p in range(4):
        scattered(16 + p, recv3, pieces[p])
        dx = total(part3, recv3, pieces[p])
        own = pl.ds(m * (4 * share) + p, share, stride=4)
        nx = normed_rows(own)
        first = jnp.mean(dx, -1, keepdims=True)
        second = jnp.mean(dx * nx, -1, keepdims=True)
        dx = scale[own, :][:, 0:1] * (dx - first - nx * second)
        for j in range(feat // 128):
            out_f32[j, pl.ds(p, share, stride=4), :] = dx[:, j * 128 : (j + 1) * 128]
    for j in range(feat // 128):
        out[:, j * 128 : (j + 1) * 128] = out_f32[j].astype(BF)

    for p in range(6):
        seq_copy(slots(p, 15), slots(p, 15), w_send.at[p], w_recv.at[p, 0], sib).wait_send()
    for step, ref in mp_sent:
        mp_copy(step, ref, ref, (m + 1) % n_mp).wait_send()
    for which in (0, 1):
        kv_copy(which, keys, keys, 0, sib).wait_send()
        ret_copy(which, keys, keys, 0, sib).wait_send()


def local(patches, w_merge1, w_merge2, w_query, w_keyval, attn_grad, sample_ids):
    n_seq, n_mp = lax.axis_size("seq"), lax.axis_size("mp")
    w1 = w_merge1.reshape(-1, w_merge1.shape[2])
    wkv = w_keyval.reshape(-1, HEAD)
    tok = attn_grad.shape[0]
    share = tok // n_mp
    feat = patches.shape[1]
    hid = w1.shape[1]
    width = n_seq * w_query.shape[0]
    qw = w_query.shape[1]
    span = N_BLOCKS * tok
    scratch = [
        pltpu.VMEM(patches.shape, BF),
        pltpu.VMEM(attn_grad.shape, BF),
        pltpu.VMEM(wkv.shape, BF),
        pltpu.VMEM(wkv.shape, F32),
        pltpu.VMEM((n_seq, *w1.shape), BF),
        pltpu.VMEM((4 * feat, hid), BF),
        pltpu.VMEM((n_seq, *w_merge2.shape), BF),
        pltpu.VMEM((width, qw), BF),
        pltpu.VMEM((width, 2 * HEAD), BF),
        pltpu.VMEM((feat // 128, 4 * tok, 128), F32),
        pltpu.VMEM((4 * tok, 128), F32),
        pltpu.VMEM((tok, hid), F32),
        pltpu.VMEM((tok, hid), BF),
        pltpu.VMEM((tok, width), BF),
        pltpu.VMEM((n_mp, share, width), BF),
        pltpu.VMEM((tok, width), BF),
        pltpu.VMEM((tok, width), BF),
        pltpu.VMEM((qw // HEAD * tok, HEAD), BF),
        pltpu.VMEM((span, HEAD), BF),
        pltpu.VMEM((span, HEAD), BF),
        pltpu.VMEM((tok, span), F32),
        pltpu.VMEM((span, HEAD), F32),
        pltpu.VMEM((span, HEAD), F32),
        pltpu.VMEM((2, 4 * tok, HEAD), BF),
        pltpu.VMEM((2, 4 * tok, HEAD), BF),
        pltpu.VMEM((2, 4, tok, HEAD), BF),
        pltpu.VMEM((2, 4, tok, HEAD), BF),
        pltpu.VMEM((2, tok, HEAD), BF),
        pltpu.VMEM((2, tok, HEAD), BF),
        pltpu.VMEM((2, tok, HEAD), BF),
        pltpu.VMEM((2, tok, HEAD), BF),
        pltpu.VMEM((tok, qw), BF),
        pltpu.VMEM((tok, 2 * HEAD), BF),
        pltpu.VMEM((tok, width), F32),
        pltpu.VMEM((tok, width), BF),
        pltpu.VMEM((n_mp, share, width), BF),
        pltpu.VMEM((tok, width), BF),
        pltpu.VMEM((tok, 4 * feat), BF),
        pltpu.VMEM((n_mp, share, 4 * feat), BF),
        pltpu.VMEM((feat // 128, 4 * share, 128), F32),
        pltpu.SemaphoreType.DMA((6,)),
        pltpu.SemaphoreType.DMA((6,)),
        pltpu.SemaphoreType.DMA((6, 4)),
        pltpu.SemaphoreType.DMA((7,)),
        pltpu.SemaphoreType.DMA((20,)),
        pltpu.SemaphoreType.DMA((20,)),
        pltpu.SemaphoreType.DMA((2,)),
        pltpu.SemaphoreType.DMA((2, 6)),
        pltpu.SemaphoreType.DMA((2,)),
        pltpu.SemaphoreType.DMA((2, 7)),
    ]
    vmem = pl.BlockSpec(memory_space=pltpu.VMEM)
    return pl.pallas_call(
        functools.partial(kernel, n_seq, n_mp),
        out_shape=jax.ShapeDtypeStruct((4 * share, feat), BF),
        in_specs=[pl.BlockSpec(memory_space=pl.ANY)] * 6 + [vmem],
        out_specs=vmem,
        scratch_shapes=scratch,
        compiler_params=pltpu.CompilerParams(
            collective_id=0, has_side_effects=True, vmem_limit_bytes=56 * 1024 * 1024
        ),
        name="merger",
    )(patches, w1, w_merge2, w_query, wkv, attn_grad, sample_ids)


def solution(mesh):
    in_specs = (
        P(("group", "seq"), None),
        P(None, "seq", "mp"),
        P("mp", "seq"),
        P("seq", "mp"),
        P("seq", None, "mp"),
        P(("group", "seq"), "mp"),
        P("group", None),
    )
    out_specs = P(("group", "seq", "mp"), None)
    return jax.shard_map(local, mesh=mesh, in_specs=in_specs, out_specs=out_specs, check_vma=False)
```

time: 154 us -> 133 us (0.86)
  the two profiles are of different devices: /device:TPU:334 before, /device:TPU:136 now
where the time goes in v3:
time: 133 us
  Pallas kernels  131 us (98%)
  local copies, waits for them, and re-layouts  1.53 us (1%)
    pallas_call x1, Pallas kernels, local(): pl.pallas_call(functools.partial(kernel, n_seq, n_mp), out_shape=jax.Shap...  131 us

profile of v3, /device:TPU:136, one launch (start us, length us, event | category | flops | bytes accessed | tf_op | source)
XLA Modules:
  0.0 133.0 jit_solution(4441028666573260944)
XLA Ops:
  0.0 131.4 %merger.1 = bf16[64,640]{1,0:T(8,128)(2,1)} custom-call(bf16[512,640]{1,0:T(8,128)(2,1)} %patches_hbm.1, bf16[160,320]{1,0:T(8,128)(2,1)} %bitcast.3, bf16[320,256]{1,0:T(8,128)(2,1)} %w2_hbm.1, bf16[256,512]{1,0:T(8,128)(2,1)} %wq_hbm.1, bf16[512,128]{1,0:T(8,128)(2,1)} %bitcast.2, bf16[128,512]{1,0:T(8,128)(2,1)} %attn_grad_hbm.1, s32[1,2048]{1,0:T(1,128)} %sample_ids.1), custom_call_target="tpu_custom_call" | custom-call | tf_op jit(solution)/shard_map/merger/pallas_call | solution.py:620
  131.4 1.5 %copy.9 = bf16[64,640]{1,0:T(8,128)(2,1)} copy(bf16[64,640]{1,0:T(8,128)(2,1)} %merger.1) | data formatting | bytes 163840

commit v4 on v3

--- a/solution.py
+++ b/solution.py
@@ -84,6 +84,7 @@
     dn_acc,
     part2,
     recv2,
+    sum2,
     dmerged,
     part3,
     recv3,
@@ -412,12 +413,12 @@
         kv_copy(which, own, block((keys, values)[which], 3), 2, up2).start()
         kv_copy(which, own, block((keys, values)[which], 1), 5, near).start()
     kv_step(1)
+    hop(WQB, 4)
     for which in (0, 1):
         ref = kv_relay.at[which]
         kv_copy(which, ref, ref, 0, sib).wait_recv()
         kv_copy(which, ref, block((keys, values)[which], 5), 4, down2).start()
     hop(WQA, 5)
-    hop(WQB, 4)
     kv_step(2)
     kv_step(3)
     kv_step(4)
@@ -507,25 +508,111 @@
             value = value + chain_recv[which, d - 1].astype(F32)
         grads_kv[:, which * HEAD : (which + 1) * HEAD] = value.astype(BF)
 
-    for g in range(4):
+    n_x = n_mp // 2
+    z, x_id = m // n_x, m % n_x
+    z_peer = (m + n_x) % n_mp
+    col_b = spans[0]
+    col_a = slice(spans[1].start, spans[3].stop)
+
+    def x_peer(o):
+        return z * n_x + (x_id + o) % n_x
+
+    def block_rows(zz, xx):
+        return rows((zz * n_x + xx) * share, share)
+
+    def rs_copy(src, dst, arrive, peer):
+        return pltpu.make_async_remote_copy(
+            src_ref=src,
+            dst_ref=dst,
+            send_sem=rs_send.at[8],
+            recv_sem=rs_recv.at[8 + arrive],
+            device_id={"mp": peer},
+            device_id_type=pl.DeviceIdType.MESH,
+        )
+
+    def rs_wait(ref, arrive):
+        rs_copy(ref, ref, arrive, z_peer).wait_recv()
+
+    for g in (1, 2, 3, 0):
         for s in range(2 * groups[g][0], 2 * groups[g][-1] + 2):
             at = slice(s * dblk, (s + 1) * dblk)
             part2[:, at] = (dn_acc[:, at] + dot_nt(grads_kv[...], wkvg[at, :])).astype(BF)
-        scatter(8 + g, part2, recv2, spans[g])
-    for g in range(4):
-        scattered(8 + g, recv2, spans[g])
+        if g > 0:
+            for xx in range(n_x):
+                rs_copy(
+                    part2.at[block_rows(1 - z, xx), spans[g]], recv2.at[xx, :, spans[g]], g, z_peer
+                ).start()
+        else:
+            for o in range(1, n_x):
+                for zz in range(2):
+                    rs_copy(
+                        part2.at[block_rows(zz, (x_id + o) % n_x), col_b],
+                        recv2.at[2 * (n_x - o) + zz, :, col_b],
+                        0,
+                        x_peer(o),
+                    ).start()
+    def sum_a(xx, at):
+        return part2[block_rows(z, xx), at].astype(F32) + recv2[xx, :, at].astype(F32)
+
+    for g in (1, 2, 3):
+        rs_wait(recv2.at[pl.ds(0, n_x), :, spans[g]], g)
+        for o in range(1, n_x):
+            sum2[o, :, spans[g]] = sum_a((x_id + o) % n_x, spans[g]).astype(BF)
+            rs_copy(sum2.at[o, :, spans[g]], recv2.at[2 * n_x - o, :, spans[g]], 4, x_peer(o)).start()
+    rs_wait(recv2.at[pl.ds(2, 2 * n_x - 2), :, col_b], 0)
+
+    def sum_b(zz):
+        value = part2[block_rows(zz, x_id), col_b].astype(F32)
+        for o in range(1, n_x):
+            value = value + recv2[2 * o + zz, :, col_b].astype(F32)
+        return value
+
+    sum2[0, :, col_b] = sum_b(1 - z).astype(BF)
+    rs_copy(sum2.at[0, :, col_b], recv2.at[0, :, col_b], 5, z_peer).start()
+    dn_a, dn_b = sum_a(x_id, col_a), sum_b(z)
+    rs_wait(recv2.at[pl.ds(n_x + 1, n_x - 1), :, col_a], 4)
+    for o in range(1, n_x):
+        dn_a = dn_a + recv2[n_x + o, :, col_a].astype(F32)
+    rs_wait(recv2.at[0, :, col_b], 5)
+    dn_b = dn_b + recv2[0, :, col_b].astype(F32)
     x = merged[mine, :].astype(F32)
     r = lax.rsqrt(jnp.mean(x * x, -1, keepdims=True) + EPSILON)
     x = x * r
-    dn = total(part2, recv2, slice(0, n_seq * dblk))
+    dn = jnp.concatenate([dn_b, dn_a], 1)
     dmerged[mine, :] = (r * (dn - x * jnp.mean(dn * x, -1, keepdims=True))).astype(BF)
-    for g in range(4):
-        spread(12 + g, dmerged, spans[g])
+
+    def ag_copy(block, at, arrive, peer):
+        ref = dmerged.at[block, at]
+        return pltpu.make_async_remote_copy(
+            src_ref=ref,
+            dst_ref=ref,
+            send_sem=rs_send.at[9],
+            recv_sem=rs_recv.at[20 + arrive],
+            device_id={"mp": peer},
+            device_id_type=pl.DeviceIdType.MESH,
+        )
+
+    ag_copy(mine, col_b, 0, z_peer).start()
+    for o in range(1, n_x):
+        ag_copy(mine, col_a, n_x - o, x_peer(o)).start()
+    ag_copy(mine, col_a, 4, z_peer).start()
+    for o in range(1, n_x):
+        ag_copy(mine, col_b, 5, x_peer(o)).start()
+    theirs = rows(z_peer * share, share)
+    ag_copy(theirs, col_b, 0, z_peer).wait_recv()
+    for o in range(1, n_x):
+        ag_copy(theirs, col_b, 5, x_peer(o)).start()
+    for o in (1, 3, 2):
+        block_of = rows(x_peer(o) * share, share)
+        ag_copy(block_of, col_a, o, z_peer).wait_recv()
+        ag_copy(block_of, col_a, 4, z_peer).start()
     acc = jnp.zeros((tok, hid), F32)
-    for g in range(4):
-        spread_done(12 + g, dmerged, spans[g])
-        for s in range(2 * groups[g][0], 2 * groups[g][-1] + 2):
-            acc = acc + dot_nt(dmerged[:, s * dblk : (s + 1) * dblk], w2g[s])
+    ag_copy(pl.ds(0, (2 * n_x - 2) * share), col_b, 5, z_peer).wait_recv()
+    for s in range(2 * groups[0][0], 2 * groups[0][-1] + 2):
+        acc = acc + dot_nt(dmerged[:, s * dblk : (s + 1) * dblk], w2g[s])
+    ag_copy(pl.ds(0, n_x * share), col_a, 4, z_peer).wait_recv()
+    for s in range(2 * groups[1][0], n_seq):
+        acc = acc + dot_nt(dmerged[:, s * dblk : (s + 1) * dblk], w2g[s])
     dhidden = (acc * gelu_grad(hidden_pre[...])).astype(BF)
     pieces = [slice(p * feat, (p + 1) * feat) for p in range(4)]
     for p in range(4):
@@ -548,6 +635,9 @@
         seq_copy(slots(p, 15), slots(p, 15), w_send.at[p], w_recv.at[p, 0], sib).wait_send()
     for step, ref in mp_sent:
         mp_copy(step, ref, ref, (m + 1) % n_mp).wait_send()
+    both = dmerged.at[pl.ds(0, (n_mp - 1) * share)]
+    rs_copy(both, both, 0, z_peer).wait_send()
+    ag_copy(pl.ds(0, (n_mp - 1) * share), slice(0, n_seq * dblk), 0, z_peer).wait_send()
     for which in (0, 1):
         kv_copy(which, keys, keys, 0, sib).wait_send()
         ret_copy(which, keys, keys, 0, sib).wait_send()
@@ -601,6 +691,7 @@
         pltpu.VMEM((tok, width), F32),
         pltpu.VMEM((tok, width), BF),
         pltpu.VMEM((n_mp, share, width), BF),
+        pltpu.VMEM((n_mp // 2, share, width), BF),
         pltpu.VMEM((tok, width), BF),
         pltpu.VMEM((tok, 4 * feat), BF),
         pltpu.VMEM((n_mp, share, 4 * feat), BF),
@@ -610,7 +701,7 @@
         pltpu.SemaphoreType.DMA((6, 4)),
         pltpu.SemaphoreType.DMA((7,)),
         pltpu.SemaphoreType.DMA((20,)),
-        pltpu.SemaphoreType.DMA((20,)),
+        pltpu.SemaphoreType.DMA((26,)),
         pltpu.SemaphoreType.DMA((2,)),
         pltpu.SemaphoreType.DMA((2, 6)),
         pltpu.SemaphoreType.DMA((2,)),

time: 133 us -> 129 us (0.970)
  the two profiles are of different devices: /device:TPU:136 before, /device:TPU:2 now
where the time goes in v4:
time: 129 us
  Pallas kernels  127 us (98%)
  local copies, waits for them, and re-layouts  1.53 us (1%)
    pallas_call x1, Pallas kernels, local(): pl.pallas_call(functools.partial(kernel, n_seq, n_mp), out_shape=jax.Shap...  127 us

profile of v4, /device:TPU:2, one launch (start us, length us, event | category | flops | bytes accessed | tf_op | source)
XLA Modules:
  0.0 128.5 jit_solution(8755788623833224124)
XLA Ops:
  0.0 127.0 %merger.1 = bf16[64,640]{1,0:T(8,128)(2,1)} custom-call(bf16[512,640]{1,0:T(8,128)(2,1)} %patches_hbm.1, bf16[160,320]{1,0:T(8,128)(2,1)} %bitcast.3, bf16[320,256]{1,0:T(8,128)(2,1)} %w2_hbm.1, bf16[256,512]{1,0:T(8,128)(2,1)} %wq_hbm.1, bf16[512,128]{1,0:T(8,128)(2,1)} %bitcast.2, bf16[128,512]{1,0:T(8,128)(2,1)} %attn_grad_hbm.1, s32[1,2048]{1,0:T(1,128)} %sample_ids.1), custom_call_target="tpu_custom_call" | custom-call | tf_op jit(solution)/shard_map/merger/pallas_call | solution.py:711
  127.0 1.5 %copy.9 = bf16[64,640]{1,0:T(8,128)(2,1)} copy(bf16[64,640]{1,0:T(8,128)(2,1)} %merger.1) | data formatting | bytes 163840

commit v5 on v4

--- a/solution.py
+++ b/solution.py
@@ -52,6 +52,7 @@
     attn_grad,
     wkv_raw,
     wkv_f32,
+    w1_raw,
     w1g,
     w1n,
     w2g,
@@ -64,7 +65,7 @@
     part,
     recv,
     merged,
-    tok_bf,
+    row_scale,
     query,
     keys,
     values,
@@ -158,7 +159,7 @@
 
     own_q = wqg.at[rows(core * rq, rq)]
     loads = [
-        pltpu.make_async_copy(w1_hbm, w1g.at[core], in_sem.at[0]),
+        pltpu.make_async_copy(w1_hbm, w1_raw, in_sem.at[0]),
         pltpu.make_async_copy(w2_hbm, w2g.at[core], in_sem.at[1]),
         pltpu.make_async_copy(patches_hbm, patches, in_sem.at[2]),
         pltpu.make_async_copy(wkv_hbm, wkv_raw, in_sem.at[3]),
@@ -168,6 +169,12 @@
     for load in loads:
         load.start()
     loads[0].wait()
+    r1 = w1_raw.shape[0]
+    full = hid // 128
+    for j in range(full):
+        w1g[core, j * r1 : (j + 1) * r1, :] = w1_raw[:, j * 128 : (j + 1) * 128]
+    tail = w1_raw[:, full * 128 :].astype(F32)
+    w1g[core, full * r1 :, :] = jnp.concatenate([tail[: r1 // 2], tail[r1 // 2 :]], 1).astype(BF)
     loads[1].wait()
     pl.semaphore_wait(barrier, 6 + n_mp - 1)
 
@@ -321,12 +328,16 @@
 
     for place, step in enumerate((0, -1, 1, -2, 2, -3, 3, 4)):
         chip = (i // 2 + n_seq // 2 + step) % (n_seq // 2)
-        a = w1g[2 * place].astype(F32)
-        b = w1g[2 * place + 1].astype(F32)
+        pair = [w1g[2 * place + c].astype(F32) for c in (0, 1)]
         for p in range(4):
-            piece = jnp.concatenate([a[p * fs : (p + 1) * fs], b[p * fs : (p + 1) * fs]], 0)
             at = pl.ds(pl.multiple_of(p * feat + 2 * fs * chip, 2 * fs), 2 * fs)
-            w1n[at, :] = piece.astype(BF)
+            for j in range(full):
+                first = j * r1 + p * fs
+                piece = jnp.concatenate([v[first : first + fs] for v in pair], 0)
+                w1n[at, j * 128 : (j + 1) * 128] = piece.astype(BF)
+            first = full * r1 + (p % 2) * fs
+            piece = jnp.concatenate([v[first : first + fs] for v in pair], 0)
+            w1n[at, full * 128 :] = piece[:, (p // 2) * 64 : (p // 2) * 64 + 64].astype(BF)
 
     acc = jnp.zeros((tok, hid), F32)
     for p in range(4):
@@ -379,11 +390,11 @@
         at = rows(c * 16, 16)
         x = merged[at, :].astype(F32)
         r = lax.rsqrt(jnp.mean(x * x, -1, keepdims=True) + EPSILON)
-        tok_bf[at, :] = (x * r).astype(BF)
+        row_scale[at, :] = jnp.broadcast_to(r, (16, 128))
 
     hop(WQB, 3)
     gathered(slots(WKV, 8), 5)
-    kv = dot(tok_bf[...], wkvg[...])
+    kv = dot(merged[...], wkvg[...]) * row_scale[:, 0:1]
     keys[0:tok, :] = kv[:, :HEAD].astype(BF)
     values[0:tok, :] = kv[:, HEAD:].astype(BF)
 
@@ -427,15 +438,13 @@
     per_kv = qw // HEAD
     for h in range(per_kv):
         at = slice(h * HEAD, (h + 1) * HEAD)
-        query[h * tok : (h + 1) * tok, :] = dot(tok_bf[...], wqg[:, at]).astype(BF)
+        query[h * tok : (h + 1) * tok, :] = (dot(merged[...], wqg[:, at]) * row_scale[...]).astype(BF)
     for which in (0, 1):
         ref = (keys, values)[which].at[0 : 5 * tok]
         kv_copy(which, ref, ref, 5, sib).wait_recv()
 
     loads[5].wait()
     score_scale = HEAD ** (-0.5)
-    dkeys[...] = jnp.zeros_like(dkeys)
-    dvalues[...] = jnp.zeros_like(dvalues)
 
     for h in range(per_kv):
         at = slice(h * HEAD, (h + 1) * HEAD)
@@ -443,15 +452,17 @@
         g = attn_grad[:, at]
         s = dot_nt(q, keys[...]) * score_scale + bias[...]
         e = jnp.exp(s - jnp.max(s, -1, keepdims=True))
-        soft = e / jnp.sum(e, -1, keepdims=True)
+        soft = e * (1.0 / jnp.sum(e, -1, keepdims=True))
         soft_bf = soft.astype(BF)
         attended = dot(soft_bf, values[...])
         delta = jnp.sum(g.astype(F32) * attended, -1, keepdims=True)
         dprob = dot_nt(g, values[...])
         ds = (soft * (dprob - delta)).astype(BF)
         dquery[:, at] = (dot(ds, keys[...]) * score_scale).astype(BF)
-        dkeys[...] += dot_tn(ds, q) * score_scale
-        dvalues[...] += dot_tn(soft_bf, g)
+        dk = dot_tn(ds, q) * score_scale
+        dv = dot_tn(soft_bf, g)
+        dkeys[...] = dk if h == 0 else dkeys[...] + dk
+        dvalues[...] = dv if h == 0 else dvalues[...] + dv
 
     grads = (dkeys, dvalues)
     back = core * sib + (1 - core) * far
@@ -659,7 +670,8 @@
         pltpu.VMEM(attn_grad.shape, BF),
         pltpu.VMEM(wkv.shape, BF),
         pltpu.VMEM(wkv.shape, F32),
-        pltpu.VMEM((n_seq, *w1.shape), BF),
+        pltpu.VMEM(w1.shape, BF),
+        pltpu.VMEM((n_seq, w1.size // 128, 128), BF),
         pltpu.VMEM((4 * feat, hid), BF),
         pltpu.VMEM((n_seq, *w_merge2.shape), BF),
         pltpu.VMEM((width, qw), BF),
@@ -671,7 +683,7 @@
         pltpu.VMEM((tok, width), BF),
         pltpu.VMEM((n_mp, share, width), BF),
         pltpu.VMEM((tok, width), BF),
-        pltpu.VMEM((tok, width), BF),
+        pltpu.VMEM((tok, 128), F32),
         pltpu.VMEM((qw // HEAD * tok, HEAD), BF),
         pltpu.VMEM((span, HEAD), BF),
         pltpu.VMEM((span, HEAD), BF),

time: 129 us -> 128 us (level)
  the two profiles are of different devices: /device:TPU:2 before, /device:TPU:8 now
where the time goes in v5:
time: 128 us
  Pallas kernels  127 us (99%)
  local copies, waits for them, and re-layouts  1.53 us (1%)
    pallas_call x1, Pallas kernels, local(): pl.pallas_call(functools.partial(kernel, n_seq, n_mp), out_shape=jax.Shap...  127 us

profile of v5, /device:TPU:8, one launch (start us, length us, event | category | flops | bytes accessed | tf_op | source)
XLA Modules:
  0.0 128.1 jit_solution(15730220180448589523)
XLA Ops:
  0.0 126.6 %merger.1 = bf16[64,640]{1,0:T(8,128)(2,1)} custom-call(bf16[512,640]{1,0:T(8,128)(2,1)} %patches_hbm.1, bf16[160,320]{1,0:T(8,128)(2,1)} %bitcast.3, bf16[320,256]{1,0:T(8,128)(2,1)} %w2_hbm.1, bf16[256,512]{1,0:T(8,128)(2,1)} %wq_hbm.1, bf16[512,128]{1,0:T(8,128)(2,1)} %bitcast.2, bf16[128,512]{1,0:T(8,128)(2,1)} %attn_grad_hbm.1, s32[1,2048]{1,0:T(1,128)} %sample_ids.1), custom_call_target="tpu_custom_call" | custom-call | tf_op jit(solution)/shard_map/merger/pallas_call | solution.py:723
  126.6 1.5 %copy.9 = bf16[64,640]{1,0:T(8,128)(2,1)} copy(bf16[64,640]{1,0:T(8,128)(2,1)} %merger.1) | data formatting | bytes 163840

commit v6 on v5

--- a/solution.py
+++ b/solution.py
@@ -392,7 +392,6 @@
         r = lax.rsqrt(jnp.mean(x * x, -1, keepdims=True) + EPSILON)
         row_scale[at, :] = jnp.broadcast_to(r, (16, 128))
 
-    hop(WQB, 3)
     gathered(slots(WKV, 8), 5)
     kv = dot(merged[...], wkvg[...]) * row_scale[:, 0:1]
     keys[0:tok, :] = kv[:, :HEAD].astype(BF)
@@ -419,16 +418,17 @@
         own = block((keys, values)[which], 0)
         kv_copy(which, own, block((keys, values)[which], 2), 1, up).start()
         kv_copy(which, own, kv_relay.at[which], 0, down2).start()
+    hop(WQB, 3)
     for which in (0, 1):
         own = block((keys, values)[which], 0)
         kv_copy(which, own, block((keys, values)[which], 3), 2, up2).start()
         kv_copy(which, own, block((keys, values)[which], 1), 5, near).start()
     kv_step(1)
-    hop(WQB, 4)
     for which in (0, 1):
         ref = kv_relay.at[which]
         kv_copy(which, ref, ref, 0, sib).wait_recv()
         kv_copy(which, ref, block((keys, values)[which], 5), 4, down2).start()
+    hop(WQB, 4)
     hop(WQA, 5)
     kv_step(2)
     kv_step(3)

time: 128 us -> 127 us (level)
  the two profiles are of different devices: /device:TPU:8 before, /device:TPU:128 now
where the time goes in v6:
time: 127 us
  Pallas kernels  126 us (99%)
  local copies, waits for them, and re-layouts  1.53 us (1%)
    pallas_call x1, Pallas kernels, local(): pl.pallas_call(functools.partial(kernel, n_seq, n_mp), out_shape=jax.Shap...  126 us

profile of v6, /device:TPU:128, one launch (start us, length us, event | category | flops | bytes accessed | tf_op | source)
XLA Modules:
  0.0 127.2 jit_solution(18160662040979223613)
XLA Ops:
  0.0 125.7 %merger.1 = bf16[64,640]{1,0:T(8,128)(2,1)} custom-call(bf16[512,640]{1,0:T(8,128)(2,1)} %patches_hbm.1, bf16[160,320]{1,0:T(8,128)(2,1)} %bitcast.3, bf16[320,256]{1,0:T(8,128)(2,1)} %w2_hbm.1, bf16[256,512]{1,0:T(8,128)(2,1)} %wq_hbm.1, bf16[512,128]{1,0:T(8,128)(2,1)} %bitcast.2, bf16[128,512]{1,0:T(8,128)(2,1)} %attn_grad_hbm.1, s32[1,2048]{1,0:T(1,128)} %sample_ids.1), custom_call_target="tpu_custom_call" | custom-call | tf_op jit(solution)/shard_map/merger/pallas_call | solution.py:723
  125.7 1.5 %copy.9 = bf16[64,640]{1,0:T(8,128)(2,1)} copy(bf16[64,640]{1,0:T(8,128)(2,1)} %merger.1) | data formatting | bytes 163840
